TPU v7x, 32 devices: a whole 2x2x4 slice. The times are simulated.
32 devices in a mesh: dp: 8 (over y, x, core), mp: 4 (over z).
Axes of the slice: x: 2, y: 2, z: 4, core: 2. Of those that a mesh axis runs over, the one named last changes fastest.
Arguments:
- block_input: bfloat16 [4096, 2048], P('dp', 'mp'), may hold values from -6 to 6
- segment_ids: int32 [8, 512], P('dp'), may hold values from 0 to 3, never falling along the last dimension, each value on 1 to 256 neighbouring positions
- expert_ids: int32 [4096, 6], P('dp'), may hold values from 0 to 15, all different within a row; in each aligned block of 512 rows (0 to 511, 512 to 1023, ...) at most 384 rows name the same one
- norm_gain: float32 [2048], replicated, may hold values from 0.5 to 1.5
- query_weight: bfloat16 [3072, 2048], P('mp', 'dp'), may hold values from -0.125 to 0.125
- latent_down: bfloat16 [576, 2048], P('mp', 'dp'), may hold values from -0.125 to 0.125
- latent_gain: float32 [512], replicated, may hold values from 0.5 to 1.5
- latent_up: bfloat16 [4096, 512], P('mp', 'dp'), may hold values from -0.25 to 0.25
- output_weight: bfloat16 [2048, 2048], P('mp', 'dp'), may hold values from -0.375 to 0.375
- moe_gain: float32 [2048], replicated, may hold values from 0.5 to 1.5
- router_weight: bfloat16 [16, 2048], P(None, 'dp'), may hold values from -0.125 to 0.125
- shared_gate: bfloat16 [2816, 2048], P('mp', 'dp'), may hold values from -0.125 to 0.125
- shared_up: bfloat16 [2816, 2048], P('mp', 'dp'), may hold values from -0.125 to 0.125
- shared_down: bfloat16 [2816, 2048], P('mp', 'dp'), may hold values from -0.109375 to 0.109375
- expert_gate: bfloat16 [32, 704, 2048], P(('dp', 'mp')), may hold values from -0.125 to 0.125
- expert_up: bfloat16 [32, 704, 2048], P(('dp', 'mp')), may hold values from -0.125 to 0.125
- expert_down: bfloat16 [32, 704, 2048], P(('dp', 'mp')), may hold values from -0.15625 to 0.15625
- output_grad: bfloat16 [4096, 2048], P('dp', 'mp'), may hold values from -6 to 6
Outputs:
- block_output: bfloat16 [4096, 2048], P('dp', 'mp')
- input_grad: float32 [4096, 2048], P('dp', 'mp')
- norm_gain_grad: float32 [2048], replicated
- query_weight_grad: float32 [3072, 2048], P('mp', 'dp')
- latent_down_grad: float32 [576, 2048], P('mp', 'dp')
- latent_gain_grad: float32 [512], replicated
- latent_up_grad: float32 [4096, 512], P('mp', 'dp')
- output_weight_grad: float32 [2048, 2048], P('mp', 'dp')
- moe_gain_grad: float32 [2048], replicated
- router_grad: float32 [16, 2048], P(None, 'dp')
- shared_gate_grad: float32 [2816, 2048], P('mp', 'dp')
- shared_up_grad: float32 [2816, 2048], P('mp', 'dp')
- shared_down_grad: float32 [2816, 2048], P('mp', 'dp')
- expert_gate_grad: float32 [32, 704, 2048], P(('dp', 'mp'))
- expert_up_grad: float32 [32, 704, 2048], P(('dp', 'mp'))
- expert_down_grad: float32 [32, 704, 2048], P(('dp', 'mp'))
Inputs may be any that keep to these rules, and one draw needn't show every extreme that they name: `expert_ids`: each token names 6 different experts. Among the tokens of one index of dp (aligned blocks of 512 tokens) no expert is named more than 384 times, and in every draw some expert is named exactly 384 times there. `segment_ids`: along each packed row the numbers never fall; a document spans 1 to 256 positions and one spans exactly that many.
All inputs are finite; a program needn't handle non-finite values.
Results may differ from a plain program's by a relative error of at most 0.018.
Values may be sent and summed in bfloat16 or wider, within the bound.
A program may use at most 384 MiB of HBM per device.

v0:
```python
import functools

import jax
import jax.numpy as jnp
from jax import lax
from jax.experimental import pallas as pl
from jax.experimental.pallas import tpu as pltpu
from jax.sharding import PartitionSpec as P

MESH = pl.DeviceIdType.MESH

H = 16
DN = 128
DR = 64
DV = 128
KVL = 512
LEN = 512


epsilon = 1e-06
negative = -1e30


def rope_tables(length, rot_width):
    half_width = rot_width // 2
    frequency = 10000.0 ** (-(2.0 / rot_width) * jnp.arange(half_width, dtype=jnp.float32))
    angles = jnp.arange(length, dtype=jnp.float32)[:, None] * frequency[None, :]
    return (jnp.cos(angles), jnp.sin(angles))


def rotate(values, cosine, sine_tab):
    half_width = values.shape[-1] // 2
    leading = values[..., :half_width]
    trailing = values[..., half_width:]
    return jnp.concatenate(
        [leading * cosine - trailing * sine_tab, trailing * cosine + leading * sine_tab], axis=-1
    )


def unrotate(values, cosine, sine_tab):
    half_width = values.shape[-1] // 2
    leading = values[..., :half_width]
    trailing = values[..., half_width:]
    return jnp.concatenate(
        [leading * cosine + trailing * sine_tab, trailing * cosine - leading * sine_tab], axis=-1
    )


def silu_grad(preact):
    sigmoid_val = jax.nn.sigmoid(preact)
    return sigmoid_val * (1.0 + preact * (1.0 - sigmoid_val))


def head_lanes(shape, heads):
    lane = lax.broadcasted_iota(jnp.int32, shape, 1)
    per_head = shape[1] // (2 * heads)
    mine = lax.rem(lane, heads * per_head) // per_head == pl.program_id(0)
    return mine.astype(jnp.float32)


def attend_forward_kernel(
    heads, scale, q_ref, q_rope_ref, keys_ref, k_rope_ref, seg_row_ref, seg_col_ref, out_ref, probs_ref
):
    width = q_ref.shape[1]
    q_rope = (q_rope_ref[...].astype(jnp.float32) * head_lanes(q_rope_ref.shape, heads)).astype(
        jnp.bfloat16
    )
    nt = (((1,), (1,)), ((), ()))
    logits = lax.dot_general(
        q_ref[...], keys_ref[:, :width], nt, preferred_element_type=jnp.float32
    )
    logits = logits + lax.dot_general(
        q_rope, k_rope_ref[...], nt, preferred_element_type=jnp.float32
    )
    row = lax.broadcasted_iota(jnp.int32, logits.shape, 0)
    column = lax.broadcasted_iota(jnp.int32, logits.shape, 1)
    kept = (seg_col_ref[...] == seg_row_ref[...]) & (column <= row)
    weights = jnp.exp(jnp.where(kept, logits * scale, negative))
    probs = (weights / jnp.sum(weights, axis=1, keepdims=True)).astype(jnp.bfloat16)
    probs_ref[0] = probs
    out_ref[...] = jnp.dot(
        probs, keys_ref[:, width:], preferred_element_type=jnp.float32
    ).astype(jnp.bfloat16)


def attend_forward(q_nope, q_rope, keys_values, k_rope, seg_row, heads, scale):
    length = q_nope.shape[0]
    whole = lambda h: (0, 0)
    mine = lambda h: (0, h)
    return pl.pallas_call(
        functools.partial(attend_forward_kernel, heads, scale),
        grid=(heads,),
        out_shape=(
            jax.ShapeDtypeStruct((length, heads * DV), jnp.bfloat16),
            jax.ShapeDtypeStruct((heads, length, length), jnp.bfloat16),
        ),
        in_specs=[
            pl.BlockSpec((length, DN), mine),
            pl.BlockSpec(q_rope.shape, whole),
            pl.BlockSpec((length, DN + DV), mine),
            pl.BlockSpec(k_rope.shape, whole),
            pl.BlockSpec((1, length), whole),
            pl.BlockSpec((length, 1), whole),
        ],
        out_specs=(
            pl.BlockSpec((length, DV), mine),
            pl.BlockSpec((1, length, length), lambda h: (h, 0, 0)),
        ),
        cost_estimate=pl.CostEstimate(
            flops=2 * heads * length * length * (DN + DV + q_rope.shape[1]),
            bytes_accessed=4 * heads * length * length,
            transcendentals=heads * length * length,
        ),
        name="attend_forward",
    )(q_nope, q_rope, keys_values, k_rope, seg_row, seg_row.T)


def attend_backward_kernel(
    heads,
    scale,
    probs_ref,
    grad_ref,
    q_ref,
    q_rope_ref,
    keys_ref,
    k_rope_ref,
    dq_ref,
    dq_rope_ref,
    dkeys_ref,
    dk_rope_ref,
):
    width = q_ref.shape[1]
    lanes = head_lanes(q_rope_ref.shape, heads)
    q_rope = (q_rope_ref[...].astype(jnp.float32) * lanes).astype(jnp.bfloat16)
    probs, grad = probs_ref[0], grad_ref[...]
    prob_grad = lax.dot_general(
        grad, keys_ref[:, width:], (((1,), (1,)), ((), ())), preferred_element_type=jnp.float32
    )
    wide = probs.astype(jnp.float32)
    row_dot = jnp.sum(wide * prob_grad, axis=1, keepdims=True)
    score_grad = (wide * (prob_grad - row_dot) * scale).astype(jnp.bfloat16)
    tn = (((0,), (0,)), ((), ()))
    dq_ref[...] = jnp.dot(
        score_grad, keys_ref[:, :width], preferred_element_type=jnp.float32
    ).astype(jnp.bfloat16)
    dq_rope = lanes * jnp.dot(score_grad, k_rope_ref[...], preferred_element_type=jnp.float32)
    dk_rope = lax.dot_general(score_grad, q_rope, tn, preferred_element_type=jnp.float32)
    dkeys_ref[:, :width] = lax.dot_general(
        score_grad, q_ref[...], tn, preferred_element_type=jnp.float32
    ).astype(jnp.bfloat16)
    dkeys_ref[:, width:] = lax.dot_general(
        probs, grad, tn, preferred_element_type=jnp.float32
    ).astype(jnp.bfloat16)

    @pl.when(pl.program_id(0) == 0)
    def _():
        dq_rope_ref[...] = dq_rope
        dk_rope_ref[...] = dk_rope

    @pl.when(pl.program_id(0) > 0)
    def _():
        dq_rope_ref[...] += dq_rope
        dk_rope_ref[...] += dk_rope


def attend_backward(probs, grad, q_nope, q_rope, keys_values, k_rope, heads, scale):
    length = q_nope.shape[0]
    whole = lambda h: (0, 0)
    mine = lambda h: (0, h)
    return pl.pallas_call(
        functools.partial(attend_backward_kernel, heads, scale),
        grid=(heads,),
        out_shape=(
            jax.ShapeDtypeStruct(q_nope.shape, jnp.bfloat16),
            jax.ShapeDtypeStruct(q_rope.shape, jnp.float32),
            jax.ShapeDtypeStruct(keys_values.shape, jnp.bfloat16),
            jax.ShapeDtypeStruct(q_rope.shape, jnp.float32),
        ),
        in_specs=[
            pl.BlockSpec((1, length, length), lambda h: (h, 0, 0)),
            pl.BlockSpec((length, DV), mine),
            pl.BlockSpec((length, DN), mine),
            pl.BlockSpec(q_rope.shape, whole),
            pl.BlockSpec((length, DN + DV), mine),
            pl.BlockSpec(k_rope.shape, whole),
        ],
        out_specs=(
            pl.BlockSpec((length, DN), mine),
            pl.BlockSpec(q_rope.shape, whole),
            pl.BlockSpec((length, DN + DV), mine),
            pl.BlockSpec(q_rope.shape, whole),
        ),
        cost_estimate=pl.CostEstimate(
            flops=2 * heads * length * length * 2 * (DN + DV + q_rope.shape[1]),
            bytes_accessed=4 * heads * length * length,
            transcendentals=0,
        ),
        name="attend_backward",
    )(probs, grad, q_nope, q_rope, keys_values, k_rope)


def expert_kernel(held, *refs):
    xs, gs = refs[:4], refs[4:8]
    mask_ref, own_ref, *weights = refs[8:13]
    refs = refs[13 + held :]
    back_same, back_other, score_ref, act_ref, gate_pre_ref, up_pre_ref, x_all, g_all = refs[:8]
    pre_gate, pre_up, grads, gate_ref, up_ref, down_ref, arrived = refs[8:]
    hidden = gate_ref.shape[0]
    nt = (((1,), (1,)), ((), ()))
    tn = (((0,), (0,)), ((), ()))
    first = pl.program_id(0) == 0
    copies = [
        pltpu.make_async_copy(weight, kept, arrived.at[i])
        for i, (weight, kept) in enumerate(zip(weights, (gate_ref, up_ref, down_ref)))
    ]

    @pl.when(first)
    def _():
        for copy in copies:
            copy.start()

    half = xs[0].shape[0]
    for part in range(2):
        rows = slice(part * half, (part + 1) * half)
        x_all[rows, :] = jnp.where(first, xs[part][...], xs[part + 2][...])
        g_all[rows, :] = jnp.where(first, gs[part][...], gs[part + 2][...])

    def arrive(i):
        @pl.when(first)
        def _():
            copies[i].wait()

    arrive(0)
    pre_gate[...] = lax.dot_general(
        gate_ref[...], x_all[...], nt, preferred_element_type=jnp.float32
    )
    arrive(1)
    pre_up[...] = lax.dot_general(up_ref[...], x_all[...], nt, preferred_element_type=jnp.float32)
    arrive(2)
    grads[...] = lax.dot_general(
        down_ref[...], g_all[...], nt, preferred_element_type=jnp.float32
    )
    mask = mask_ref[...]
    pick_exp = jnp.exp(jnp.where(mask > 0, pre_up[hidden:, :], negative))
    share = jnp.sum(pick_exp * own_ref[...], axis=0, keepdims=True) / jnp.sum(
        pick_exp, axis=0, keepdims=True
    )
    step = 32 if hidden % 32 == 0 else 16

    def body(i, score):
        rows = pl.ds(pl.multiple_of(i * step, step), step)
        gate_in, up_in, grad = pre_gate[rows, :], pre_up[rows, :], grads[rows, :]
        sig = jax.nn.sigmoid(gate_in)
        silu = gate_in * sig
        activation = silu * up_in
        scaled = grad * share
        act_ref[rows, :] = (activation * share).astype(jnp.bfloat16)
        gate_pre_ref[rows, :] = (scaled * up_in * (sig * (1.0 + gate_in * (1.0 - sig)))).astype(
            jnp.bfloat16
        )
        up_pre_ref[rows, :] = (scaled * silu).astype(jnp.bfloat16)
        return score + jnp.sum(activation * grad, axis=0, keepdims=True)

    score_ref[...] = lax.fori_loop(
        0, hidden // step, body, jnp.zeros((1, x_all.shape[0]), jnp.float32)
    )
    width = 512
    for low in range(0, gate_ref.shape[1], width):
        columns = slice(low, low + width)
        back = lax.dot_general(
            gate_pre_ref[...], gate_ref[:, columns], tn, preferred_element_type=jnp.float32
        ) + lax.dot_general(
            up_pre_ref[...], up_ref[:hidden, columns], tn, preferred_element_type=jnp.float32
        )
        back = back.astype(jnp.bfloat16)

        @pl.when(first)
        def _(back=back, columns=columns):
            back_same[:, columns] = back

        @pl.when(jnp.logical_not(first))
        def _(back=back, columns=columns):
            back_other[:, columns] = back


def expert_rows(k, chips, rows, grads, mask, own, gate, up_router, down, held):
    half, width = rows[0].shape
    tokens = 2 * half
    hidden = gate.shape[0]
    whole = lambda shape: pl.BlockSpec(shape, lambda i: (0, 0), pipeline_mode=pl.Buffered(1))
    bf = jnp.bfloat16
    total = 2 * chips * tokens
    slab = pl.BlockSpec((hidden, tokens), lambda i: (0, 2 * k + i))
    lines = pl.BlockSpec((tokens, width), lambda i: (2 * k + i, 0))
    return pl.pallas_call(
        functools.partial(expert_kernel, len(held)),
        grid=(2,),
        out_shape=(
            jax.ShapeDtypeStruct((tokens, width), bf),
            jax.ShapeDtypeStruct((tokens, width), bf),
            jax.ShapeDtypeStruct((1, 2 * tokens), jnp.float32),
            jax.ShapeDtypeStruct((hidden, total), bf),
            jax.ShapeDtypeStruct((hidden, total), bf),
            jax.ShapeDtypeStruct((hidden, total), bf),
            jax.ShapeDtypeStruct((total, width), bf),
            jax.ShapeDtypeStruct((total, width), bf),
        ),
        in_specs=[
            *[whole((half, width))] * 8,
            pl.BlockSpec((mask.shape[0], tokens), lambda i: (0, i)),
            whole(own.shape),
            *[pl.BlockSpec(memory_space=pl.ANY)] * (3 + len(held)),
        ],
        out_specs=(
            whole((tokens, width)),
            whole((tokens, width)),
            pl.BlockSpec((1, tokens), lambda i: (0, i)),
            slab,
            slab,
            slab,
            lines,
            lines,
        ),
        scratch_shapes=[
            pltpu.VMEM((hidden, tokens), jnp.float32),
            pltpu.VMEM((up_router.shape[0], tokens), jnp.float32),
            pltpu.VMEM((hidden, tokens), jnp.float32),
            pltpu.VMEM(gate.shape, bf),
            pltpu.VMEM(up_router.shape, bf),
            pltpu.VMEM(down.shape, bf),
            pltpu.SemaphoreType.DMA((3,)),
        ],
        input_output_aliases={13 + i: 3 + i for i in range(len(held))},
        cost_estimate=pl.CostEstimate(
            flops=2 * 2 * tokens * hidden * width * 5,
            bytes_accessed=2 * (3 * hidden * width + 10 * tokens * width),
            transcendentals=2 * tokens * hidden,
        ),
        name="expert_rows",
    )(*rows, *grads, mask, own, gate, up_router, down, *held)


def full_rows(piece_rows):
    return lax.all_gather(piece_rows, "mp", axis=1, tiled=True)


def mp_share(partial_value):
    return lax.psum_scatter(
        partial_value.astype(jnp.bfloat16), "mp", scatter_dimension=1, tiled=True
    ).astype(jnp.float32)


def ring_order(dp_count):
    chips = dp_count // 2
    return list(range(chips // 2)) + list(range(chips - 1, chips // 2 - 1, -1))


def ring_neighbours(dp_count):
    order = ring_order(dp_count)
    chips = len(order)
    place = lax.axis_index("dp")
    chip, core = place // 2, place % 2
    pos = jnp.where(chip < chips // 2, chip, chips // 2 + chips - 1 - chip)

    def device_at(p):
        p = lax.rem(p + 2 * chips, chips)
        c = jnp.where(p < chips // 2, p, chips // 2 + chips - 1 - p)
        return 2 * c + core

    return place, pos, core, device_at


def gather_kernel(dp_count, mp_count, axes, has_rows, *refs):
    count = len(axes)
    if not has_rows:
        refs = (None, *refs[:count], None, *refs[count:])
    rows_ref, parts = refs[0], refs[1 : 1 + count]
    rows_out, wholes = refs[1 + count], refs[2 + count : 2 + 2 * count]
    send, receive, local, line_send, line_receive, line_local = refs[2 + 2 * count :]
    chips = dp_count // 2
    reach = chips // 2
    place, pos, core, device_at = ring_neighbours(dp_count)
    line = lax.axis_index("mp")
    on, back = device_at(pos + 1), device_at(pos - 1)
    other = place + 1 - 2 * core

    barrier = pltpu.get_barrier_semaphore()
    for target in (on, back, other):
        pl.semaphore_signal(barrier, device_id={"dp": target}, device_id_type=MESH)

    waits = 3
    if has_rows:

        @pl.when(line > 0)
        def _():
            pl.semaphore_signal(barrier, device_id={"mp": line - 1}, device_id_type=MESH)

        @pl.when(line < mp_count - 1)
        def _():
            pl.semaphore_signal(barrier, device_id={"mp": line + 1}, device_id_type=MESH)

        waits = 3 + (line > 0).astype(jnp.int32) + (line < mp_count - 1).astype(jnp.int32)
    pl.semaphore_wait(barrier, waits)

    width = rows_ref.shape[1] if has_rows else 0

    def columns(owner):
        return rows_out.at[:, pl.ds(pl.multiple_of(owner * width, width), width)]

    def line_copy(way, hop, source, owner):
        target = line + 1 if way == 0 else line - 1
        return pltpu.make_async_remote_copy(
            source,
            columns(owner),
            line_send.at[way, hop],
            line_receive.at[way, hop],
            device_id={"mp": target},
            device_id_type=MESH,
        )

    ends = (line < mp_count - 1, line > 0)

    def holds(way, hop):
        return line >= hop if way == 0 else line + hop <= mp_count - 1

    def owner_of(way, hop):
        return jnp.clip(line - hop if way == 0 else line + hop, 0, mp_count - 1)

    if has_rows:
        for way in range(2):

            @pl.when(ends[way])
            def _(way=way):
                line_copy(way, 0, rows_ref, line).start()

        keep_rows = pltpu.make_async_copy(rows_ref, columns(line), line_local)
        keep_rows.start()

    def block(i, owner, low, high):
        size = parts[i].shape[axes[i]]
        start = pl.multiple_of(owner * size, size)
        if axes[i] == 1:
            return wholes[i].at[pl.ds(low, high - low), pl.ds(start, size)]
        return wholes[i].at[pl.ds(start + low, high - low), :]

    def split(i, piece):
        rows = parts[i].shape[0]
        middle = rows // 32 * 16
        return ((0, rows), (0, middle), (middle, rows))[piece]

    def ring_copy(i, slot, source, owner, piece, target):
        low, high = split(i, piece)
        if source is None:
            source = block(i, owner, low, high)
        return pltpu.make_async_remote_copy(
            source,
            block(i, owner, low, high),
            send.at[i, slot],
            receive.at[i, slot],
            device_id={"dp": target},
            device_id_type=MESH,
        )

    def empty(i, piece):
        low, high = split(i, piece)
        return low == high

    started, kept = [], []
    for i in range(count):
        for way, target in ((0, on), (1, back)):
            piece = 0 if reach > 1 else 1 + way
            if not empty(i, piece):
                low, high = split(i, piece)
                copy = ring_copy(
                    i, way * reach, parts[i].at[pl.ds(low, high - low), :], place, piece, target
                )
                copy.start()
                started.append(copy)
        copy = ring_copy(i, 2 * reach, parts[i], place, 0, other)
        copy.start()
        started.append(copy)
        copy = pltpu.make_async_copy(
            parts[i], block(i, place, 0, parts[i].shape[0]), local.at[i]
        )
        copy.start()
        kept.append(copy)

    def line_step(hop):
        for way in range(2):

            @pl.when(holds(way, hop))
            def _(way=way):
                line_copy(way, hop - 1, rows_ref, owner_of(way, hop)).wait_recv()

            if hop < mp_count - 1:

                @pl.when(holds(way, hop) & ends[way])
                def _(way=way):
                    owner = owner_of(way, hop)
                    line_copy(way, hop, columns(owner), owner).start()

    def ring_step(i, hop):
        for way, target in ((0, on), (1, back)):
            piece = 0 if hop < reach else 1 + way
            if empty(i, piece):
                continue
            owner = device_at(pos - hop if way == 0 else pos + hop)
            ring_copy(i, way * reach + hop - 1, None, owner, piece, other).wait_recv()
            if hop < reach:
                ahead = 0 if hop + 1 < reach else 1 + way
                if not empty(i, ahead):
                    copy = ring_copy(i, way * reach + hop, None, owner, ahead, target)
                    copy.start()
                    started.append(copy)
            copy = ring_copy(i, 2 * reach + 1 + way * reach + hop - 1, None, owner, piece, other)
            copy.start()
            started.append(copy)

    line_hops = list(range(1, mp_count)) if has_rows else []
    for hop in range(1, reach + 1):
        for i in range(count):
            ring_step(i, hop)
        if line_hops:
            line_step(line_hops.pop(0))
    for hop in line_hops:
        line_step(hop)

    for i in range(count):
        twin = place + 1 - 2 * core
        ring_copy(i, 2 * reach, parts[i], twin, 0, other).wait_recv()
        for hop in range(1, reach + 1):
            for way in range(2):
                piece = 0 if hop < reach else 1 + way
                if empty(i, piece):
                    continue
                owner = device_at(pos - hop if way == 0 else pos + hop) + 1 - 2 * core
                ring_copy(
                    i, 2 * reach + 1 + way * reach + hop - 1, None, owner, piece, other
                ).wait_recv()
    for copy in started:
        copy.wait_send()
    for copy in kept:
        copy.wait()
    if not has_rows:
        return
    for way in range(2):

        @pl.when(ends[way])
        def _(way=way):
            line_copy(way, 0, rows_ref, line).wait_send()

        for hop in range(1, mp_count - 1):

            @pl.when(holds(way, hop) & ends[way])
            def _(way=way, hop=hop):
                owner = owner_of(way, hop)
                line_copy(way, hop, columns(owner), owner).wait_send()

    keep_rows.wait()


def gather_all(rows, parts, axes, collective_id):
    dp_count, mp_count = lax.axis_size("dp"), lax.axis_size("mp")
    arrays = [part for part in (rows, *parts) if part is not None]
    shapes = [
        jax.ShapeDtypeStruct(
            tuple(s * dp_count if a == axis else s for a, s in enumerate(part.shape)), part.dtype
        )
        for part, axis in zip(parts, axes)
    ]
    semaphores = [
        pltpu.SemaphoreType.DMA((len(parts), 4 * (dp_count // 4) + 1)),
        pltpu.SemaphoreType.DMA((len(parts), 4 * (dp_count // 4) + 1)),
        pltpu.SemaphoreType.DMA((len(parts),)),
        pltpu.SemaphoreType.DMA((2, mp_count)),
        pltpu.SemaphoreType.DMA((2, mp_count)),
        pltpu.SemaphoreType.DMA,
    ]
    if rows is not None:
        shapes.insert(
            0, jax.ShapeDtypeStruct((rows.shape[0], rows.shape[1] * mp_count), rows.dtype)
        )
    moved = 2 * sum(shape.size for shape in shapes)
    return pl.pallas_call(
        functools.partial(gather_kernel, dp_count, mp_count, tuple(axes), rows is not None),
        out_shape=shapes,
        in_specs=[pl.BlockSpec(memory_space=pltpu.VMEM)] * len(arrays),
        out_specs=[pl.BlockSpec(memory_space=pl.ANY)] * len(arrays),
        scratch_shapes=semaphores,
        compiler_params=pltpu.CompilerParams(collective_id=collective_id, has_side_effects=True),
        cost_estimate=pl.CostEstimate(flops=0, bytes_accessed=16 * moved, transcendentals=0),
        name="gather_all",
    )(*arrays)


def small_total_kernel(dp_count, mp_count, value_ref, total_ref, ring, line, part, send, receive, line_send, line_receive):
    place, spot = lax.axis_index("dp"), lax.axis_index("mp")
    barrier = pltpu.get_barrier_semaphore()
    ring_targets = [lax.rem(place + shift, dp_count) for shift in range(1, dp_count)]
    line_targets = [lax.rem(spot + shift, mp_count) for shift in range(1, mp_count)]
    for target in ring_targets:
        pl.semaphore_signal(barrier, device_id={"dp": target}, device_id_type=MESH)
    for target in line_targets:
        pl.semaphore_signal(barrier, device_id={"mp": target}, device_id_type=MESH)
    pl.semaphore_wait(barrier, dp_count + mp_count - 2)
    copies = []
    for shift, target in enumerate(ring_targets):
        copies.append(
            pltpu.make_async_remote_copy(
                value_ref,
                ring.at[place],
                send.at[shift],
                receive.at[shift],
                device_id={"dp": target},
                device_id_type=MESH,
            )
        )
    for copy in copies:
        copy.start()
    ring[place] = value_ref[...]
    for copy in copies:
        copy.wait()
    total = ring[0]
    for d in range(1, dp_count):
        total = total + ring[d]
    part[...] = total
    copies = []
    for shift, target in enumerate(line_targets):
        copies.append(
            pltpu.make_async_remote_copy(
                part,
                line.at[spot],
                line_send.at[shift],
                line_receive.at[shift],
                device_id={"mp": target},
                device_id_type=MESH,
            )
        )
    for copy in copies:
        copy.start()
    line[spot] = total
    for copy in copies:
        copy.wait()
    total = line[0]
    for m in range(1, mp_count):
        total = total + line[m]
    total_ref[...] = total


def small_total(value, collective_id):
    dp_count, mp_count = lax.axis_size("dp"), lax.axis_size("mp")
    return pl.pallas_call(
        functools.partial(small_total_kernel, dp_count, mp_count),
        out_shape=jax.ShapeDtypeStruct(value.shape, value.dtype),
        in_specs=[pl.BlockSpec(memory_space=pltpu.VMEM)],
        out_specs=pl.BlockSpec(memory_space=pltpu.VMEM),
        scratch_shapes=[
            pltpu.VMEM((dp_count, *value.shape), value.dtype),
            pltpu.VMEM((mp_count, *value.shape), value.dtype),
            pltpu.VMEM(value.shape, value.dtype),
            pltpu.SemaphoreType.DMA((dp_count - 1,)),
            pltpu.SemaphoreType.DMA((dp_count - 1,)),
            pltpu.SemaphoreType.DMA((mp_count - 1,)),
            pltpu.SemaphoreType.DMA((mp_count - 1,)),
        ],
        compiler_params=pltpu.CompilerParams(collective_id=collective_id, has_side_effects=True),
        cost_estimate=pl.CostEstimate(flops=0, bytes_accessed=1 << 22, transcendentals=0),
        name="small_total",
    )(value)


def ring_move(values, step):
    order = ring_order(lax.axis_size("dp"))
    chips = len(order)
    pairs = [
        (2 * chip + core, 2 * order[(pos + step) % chips] + core)
        for pos, chip in enumerate(order)
        for core in range(2)
    ]
    return lax.ppermute(values, "dp", pairs)


def core_swap(values):
    return lax.ppermute(values, "dp", [(i, i ^ 1) for i in range(lax.axis_size("dp"))])


def direct_move(values, step, swap):
    order = ring_order(lax.axis_size("dp"))
    chips = len(order)
    pairs = [
        (2 * chip + core, 2 * order[(pos + step) % chips] + (core ^ swap))
        for pos, chip in enumerate(order)
        for core in range(2)
    ]
    return lax.ppermute(values, "dp", pairs)


def spread_pairs(own):
    chips = lax.axis_size("dp") // 2
    half = own.shape[0] // 32 * 16
    same = [None] * chips
    same[0] = ahead = behind = own
    for step in range(1, chips // 2):
        ahead = same[step] = ring_move(ahead, 1)
        behind = same[chips - step] = ring_move(behind, -1)
    ends = [ring_move(ahead[:half], 1), ring_move(behind[half:], -1)]
    same[chips // 2] = jnp.concatenate(ends, axis=0)
    return [(rows, core_swap(rows)) for rows in same]


def spread_halves(own):
    chips = lax.axis_size("dp") // 2
    half = own.shape[0] // 2
    same = [None] * chips
    same[0] = ahead = behind = [own[:half], own[half:]]
    for step in range(1, chips // 2):
        ahead = same[step] = [ring_move(part, 1) for part in ahead]
        behind = same[chips - step] = [ring_move(part, -1) for part in behind[::-1]][::-1]
    same[chips // 2] = [ring_move(ahead[0], 1), ring_move(behind[1], -1)]
    return [parts + [core_swap(part) for part in parts] for parts in same]


def add_bf(left, right):
    return (left.astype(jnp.float32) + right.astype(jnp.float32)).astype(jnp.bfloat16)


def collect(pairs):
    chips = len(pairs)
    half = pairs[0][0].shape[0] // 2
    far = add_bf(pairs[chips // 2][0], core_swap(pairs[chips // 2][1]))
    merged = [add_bf(same, core_swap(other)) for same, other in pairs]
    carry_back, carry_on = ring_move(far[:half], -1), ring_move(far[half:], 1)
    for step in range(chips // 2 - 1, 0, -1):
        back, on = merged[step], merged[chips - step]
        if step == chips // 2 - 1:
            back = jnp.concatenate([add_bf(back[:half], carry_back), back[half:]], axis=0)
            on = jnp.concatenate([on[:half], add_bf(on[half:], carry_on)], axis=0)
        else:
            back, on = add_bf(back, carry_back), add_bf(on, carry_on)
        carry_back, carry_on = ring_move(back, -1), ring_move(on, 1)
    total = merged[0].astype(jnp.float32) + carry_back.astype(jnp.float32)
    return total + carry_on.astype(jnp.float32)


def relative_devices():
    dp_count = lax.axis_size("dp")
    _, pos, core, device_at = ring_neighbours(dp_count)
    places = []
    for k in range(dp_count // 2):
        same = device_at(pos - k)
        places.append((same, same + 1 - 2 * core))
    return places


def assemble_kernel(parts, places_ref, *refs):
    pieces, wholes = refs[: len(refs) - parts], refs[len(refs) - parts :]
    width = pieces[0].shape[1]
    for part in range(parts):

        @pl.when(pl.program_id(0) == part)
        def _(part=part):
            for i, piece in enumerate(pieces):
                start = pl.multiple_of(places_ref[i] * width, width)
                wholes[part][:, pl.ds(start, width)] = piece[...]


def assemble(pieces, places, parts):
    rows, width = pieces[0].shape[0] // parts, pieces[0].shape[1]
    whole = (rows, width * len(pieces))
    return pl.pallas_call(
        functools.partial(assemble_kernel, parts),
        grid_spec=pltpu.PrefetchScalarGridSpec(
            num_scalar_prefetch=1,
            grid=(parts,),
            in_specs=[pl.BlockSpec((rows, width), lambda i, p: (i, 0))] * len(pieces),
            out_specs=[pl.BlockSpec(whole, lambda i, p: (0, 0), pipeline_mode=pl.Buffered(1))]
            * parts,
        ),
        out_shape=[jax.ShapeDtypeStruct(whole, pieces[0].dtype)] * parts,
        cost_estimate=pl.CostEstimate(
            flops=0, bytes_accessed=8 * parts * whole[0] * whole[1], transcendentals=0
        ),
        name="assemble",
    )(places, *pieces)


def weight_grads(rows, cotangents, places):
    whole = jnp.dot(rows.T, cotangents, preferred_element_type=jnp.float32).astype(
        jnp.bfloat16
    )
    width = whole.shape[0] // lax.axis_size("dp")
    pairs = [
        tuple(lax.dynamic_slice_in_dim(whole, place * width, width) for place in pair)
        for pair in places
    ]
    return collect(pairs)


def line_share(partial_value):
    count = lax.axis_size("mp")
    spot = lax.axis_index("mp")
    width = partial_value.shape[1] // count
    rounded = partial_value.astype(jnp.bfloat16)
    total = lax.dynamic_slice_in_dim(partial_value, spot * width, width, axis=1)
    for shift in range(1, count):
        target = lax.rem(spot + shift, count)
        piece = lax.ppermute(
            lax.dynamic_slice_in_dim(rounded, target * width, width, axis=1),
            "mp",
            [(i, (i + shift) % count) for i in range(count)],
        )
        total = total + piece.astype(jnp.float32)
    return total


def line_total(partial_value):
    count = lax.axis_size("mp")
    total = partial_value
    for shift in range(1, count):
        total = total + lax.ppermute(
            partial_value, "mp", [(i, (i + shift) % count) for i in range(count)]
        )
    return total


def shards(
    block_input,
    segment_ids,
    expert_ids,
    norm_gain,
    query_weight,
    latent_down,
    latent_gain,
    latent_up,
    output_weight,
    moe_gain,
    router_weight,
    shared_gate,
    shared_up,
    shared_down,
    expert_gate,
    expert_up,
    expert_down,
    output_grad,
):
    model_width = norm_gain.shape[0]
    tokens_here = block_input.shape[0]
    share_width = block_input.shape[1]
    mp_count = lax.axis_size("mp")
    mp_place = lax.axis_index("mp")
    dp_count = lax.axis_size("dp")
    heads_here = H // mp_count
    experts_all = router_weight.shape[0]
    experts_group = experts_all // dp_count
    chips = dp_count // 2
    own_expert = lax.axis_index("dp") * experts_group + mp_place // 2
    expert_places = jnp.arange(experts_all, dtype=jnp.int32)
    own_gate = expert_gate[0]
    own_up = expert_up[0]
    own_down = expert_down[0]
    cosine, sine_tab = rope_tables(LEN, DR)
    inputs = block_input.astype(jnp.float32)
    gain_one = lax.dynamic_slice_in_dim(norm_gain, mp_place * share_width, share_width)
    per_head = query_weight.reshape(heads_here, DN + DR, -1)
    query_rows = jnp.concatenate(
        [
            per_head[:, :DN].reshape(heads_here * DN, -1),
            per_head[:, DN : DN + DR // 2].reshape(heads_here * DR // 2, -1),
            per_head[:, DN + DR // 2 :].reshape(heads_here * DR // 2, -1),
        ],
        axis=0,
    )
    gathered = gather_all(
        block_input,
        (query_rows, latent_down, latent_up.T, output_weight, router_weight),
        (1, 1, 0, 1, 1),
        1,
    )
    inputs_full = gathered[0].astype(jnp.float32)
    query_w, down_w, up_wt, out_w, router_w = gathered[1:]
    scale_one = lax.rsqrt(jnp.mean(inputs_full * inputs_full, axis=1, keepdims=True) + epsilon)
    normed = (inputs_full * scale_one * norm_gain).astype(jnp.bfloat16)
    places = relative_devices()
    late_ids, _ = lax.optimization_barrier((expert_ids, gathered[0]))
    picked_mask = jnp.max((late_ids[..., None] == expert_places).astype(jnp.float32), axis=1)
    mask_pairs = spread_pairs(picked_mask)
    shared_parts, _ = lax.optimization_barrier(
        (jnp.concatenate([shared_gate, shared_up, shared_down], axis=0), gathered[0])
    )
    shared_pieces = [piece for pair in spread_pairs(shared_parts) for piece in pair]
    hidden_here = shared_gate.shape[0]
    places_flat = jnp.stack([place for pair in places for place in pair]).astype(jnp.int32)
    sgate_w, sup_w, sdown_w = assemble(shared_pieces, places_flat, 3)
    late_grad, _ = lax.optimization_barrier((output_grad, gathered[0]))
    grad_full = full_rows(late_grad)
    grad_pairs = spread_halves(grad_full)
    nope_width, rope_width = heads_here * DN, heads_here * DR
    query_all = jnp.dot(normed, query_w.T, preferred_element_type=jnp.float32)
    cosines, sines = jnp.tile(cosine, (1, heads_here)), jnp.tile(sine_tab, (1, heads_here))
    query_nope = query_all[:, :nope_width].astype(jnp.bfloat16)
    query_rope = rotate(query_all[:, nope_width:], cosines, sines).astype(jnp.bfloat16)
    score_scale = (DN + DR) ** (-0.5)
    latent_part = jnp.dot(normed, down_w.T, preferred_element_type=jnp.float32).astype(
        jnp.bfloat16
    )
    latent = full_rows(latent_part).astype(jnp.float32)
    latent_main = latent[:, :KVL]
    scale_lat = lax.rsqrt(jnp.mean(latent_main * latent_main, axis=-1, keepdims=True) + epsilon)
    latent_normed = (latent_main * scale_lat * latent_gain).astype(jnp.bfloat16)
    key_rope = rotate(latent[:, KVL:], cosine, sine_tab).astype(jnp.bfloat16)
    key_rope = jnp.concatenate(
        [key_rope[:, : DR // 2]] * heads_here + [key_rope[:, DR // 2 :]] * heads_here, axis=1
    )
    keys_values = jnp.dot(latent_normed, up_wt, preferred_element_type=jnp.float32).astype(
        jnp.bfloat16
    )
    attended_flat, probs = attend_forward(
        query_nope, query_rope, keys_values, key_rope, segment_ids, heads_here, score_scale
    )
    attended_part = jnp.dot(attended_flat, out_w, preferred_element_type=jnp.float32).astype(
        jnp.bfloat16
    )
    attended_sum = mp_share(attended_part)
    residual = inputs + attended_sum
    residual_rounded = residual.astype(jnp.bfloat16)
    gain_two = lax.dynamic_slice_in_dim(moe_gain, mp_place * share_width, share_width)
    residual_full = full_rows(residual_rounded)
    residual_full = residual_full.astype(jnp.float32)
    scale_two = lax.rsqrt(
        jnp.mean(residual_full * residual_full, axis=1, keepdims=True) + epsilon
    )
    moe_in = (residual_full * scale_two * moe_gain).astype(jnp.bfloat16)
    row_pairs = spread_halves(moe_in)
    router_logits = jnp.dot(moe_in, router_w.T, preferred_element_type=jnp.float32)

    def masked_gates(logits, mask):
        pick_exp = jnp.exp(jnp.where(mask > 0, logits, negative))
        return pick_exp / jnp.sum(pick_exp, axis=-1, keepdims=True)

    gate_prob = masked_gates(router_logits, picked_mask)
    shared_g = jnp.dot(moe_in, sgate_w.T, preferred_element_type=jnp.float32)
    shared_u = jnp.dot(moe_in, sup_w.T, preferred_element_type=jnp.float32)
    shared_act = (jax.nn.silu(shared_g) * shared_u).astype(jnp.bfloat16)
    shared_part = jnp.dot(shared_act, sdown_w, preferred_element_type=jnp.float32)
    up_router = jnp.concatenate([own_up, router_w], axis=0)
    own_column = (expert_places == own_expert).astype(jnp.float32)[:, None]
    backs, gate_grads, held = [None] * chips, [None] * chips, ()
    visits = [0]
    for hop in range(1, chips // 2):
        visits += [hop, chips - hop]
    visits.insert(len(visits) - 1, chips // 2)
    for k in visits:
        done = expert_rows(
            k,
            chips,
            row_pairs[k],
            grad_pairs[k],
            jnp.concatenate(mask_pairs[k]).T,
            own_column,
            own_gate,
            up_router,
            own_down,
            held,
        )
        *back, gate_grads[k] = done[:3]
        backs[k], held = tuple(back), done[3:]
    routed_back = collect(backs)
    act_late, _ = lax.optimization_barrier((held[0], routed_back))
    tokens_pair = 2 * tokens_here

    def out_rows(low):
        return jnp.dot(
            act_late[:, low : low + tokens_here].T,
            own_down,
            preferred_element_type=jnp.float32,
        ).astype(jnp.bfloat16)

    out_pairs = [
        (out_rows(k * tokens_pair), out_rows(k * tokens_pair + tokens_here))
        for k in range(chips)
    ]
    act_all, gate_pre_all, up_pre_all, rows_all, grads_all = held
    expert_down_grad = jnp.dot(act_all, grads_all, preferred_element_type=jnp.float32)[None]
    expert_gate_grad = jnp.dot(
        gate_pre_all, rows_all, preferred_element_type=jnp.float32
    )[None]
    expert_up_grad = jnp.dot(up_pre_all, rows_all, preferred_element_type=jnp.float32)[None]
    gate_grads, _ = lax.optimization_barrier((gate_grads, routed_back))
    order = jnp.array(ring_order(dp_count), jnp.int32)
    dp_place = lax.axis_index("dp")
    ring_place = jnp.argmax((order == dp_place // 2).astype(jnp.int32)).astype(jnp.int32)
    gate_grad = jnp.zeros((tokens_here, experts_all), jnp.float32)
    for k, both in enumerate(gate_grads):
        chip_from = jnp.sum(
            jnp.where(jnp.arange(chips) == (ring_place + k) % chips, order, 0)
        )
        for swap in range(2):
            piece = both[0, swap * tokens_here : (swap + 1) * tokens_here]
            if k or swap:
                piece = direct_move(piece, -k, swap)
            device_from = 2 * chip_from + (dp_place % 2 if swap == 0 else 1 - dp_place % 2)
            expert_from = device_from * experts_group + mp_place // 2
            gate_grad = gate_grad + piece[:, None] * (expert_places == expert_from).astype(
                jnp.float32
            )
    gate_grad = line_total(gate_grad)
    routed_part = collect(out_pairs)
    moe_total = mp_share(shared_part + routed_part)
    block_output = (residual + moe_total).astype(jnp.bfloat16)
    logit_grad = (
        gate_prob * (gate_grad - jnp.sum(gate_prob * gate_grad, axis=-1, keepdims=True))
    ).astype(jnp.bfloat16)
    router_back = jnp.dot(logit_grad, router_w, preferred_element_type=jnp.float32)
    shared_act_grad = jnp.dot(grad_full, sdown_w.T, preferred_element_type=jnp.float32)
    shared_gate_pre = (shared_act_grad * shared_u * silu_grad(shared_g)).astype(jnp.bfloat16)
    shared_up_pre = (shared_act_grad * jax.nn.silu(shared_g)).astype(jnp.bfloat16)
    moe_late, grad_late, shared_late, _ = lax.optimization_barrier(
        (
            moe_in,
            grad_full,
            (shared_act, shared_gate_pre, shared_up_pre, logit_grad),
            routed_back,
        )
    )
    sdown_grad = weight_grads(grad_late, shared_late[0], places)
    moe_rows_grad = weight_grads(moe_late, jnp.concatenate(shared_late[1:], axis=1), places)
    shared_back = jnp.dot(
        shared_gate_pre, sgate_w, preferred_element_type=jnp.float32
    ) + jnp.dot(shared_up_pre, sup_w, preferred_element_type=jnp.float32)
    router_mine = lax.dynamic_slice_in_dim(router_back, mp_place * share_width, share_width, axis=1)
    back_share = mp_share(shared_back + routed_back)
    moe_in_grad = back_share + router_mine
    moe_in_grad_bf = moe_in_grad.astype(jnp.bfloat16)
    back_full = full_rows(moe_in_grad_bf)
    back_full = back_full.astype(jnp.float32)
    moe_gain_part = jnp.sum(back_full * residual_full * scale_two, axis=0)
    stat_two = jnp.mean(back_full * residual_full * moe_gain, axis=1, keepdims=True)
    residual_grad = (
        output_grad.astype(jnp.float32)
        + scale_two * gain_two * moe_in_grad
        - residual * scale_two**3 * stat_two
    )
    residual_bf = (
        grad_full.astype(jnp.float32)
        + scale_two * moe_gain * back_full
        - residual_full * scale_two**3 * stat_two
    ).astype(jnp.bfloat16)
    out_w_grad = weight_grads(residual_bf, attended_flat, places)
    attended_grad = jnp.dot(residual_bf, out_w.T, preferred_element_type=jnp.float32).astype(
        jnp.bfloat16
    )
    dq_nope, dq_rope, kv_grad, dk_ropes = attend_backward(
        probs,
        attended_grad,
        query_nope,
        query_rope,
        keys_values,
        key_rope,
        heads_here,
        score_scale,
    )
    query_grad = jnp.concatenate(
        [dq_nope, unrotate(dq_rope, cosines, sines).astype(jnp.bfloat16)], axis=1
    )
    dk_rope = jnp.sum(dk_ropes.reshape(-1, 2, heads_here, DR // 2), axis=2).reshape(-1, DR)
    up_w_grad = weight_grads(latent_normed, kv_grad, places)
    normed_lat_grad = jnp.dot(kv_grad, up_wt.T, preferred_element_type=jnp.float32)
    latent_gain_part = jnp.sum(normed_lat_grad * latent_main * scale_lat, axis=0)
    main_grad = scale_lat * latent_gain * normed_lat_grad - latent_main * scale_lat**3 * jnp.mean(
        normed_lat_grad * latent_main * latent_gain, axis=-1, keepdims=True
    )
    rope_grad = unrotate(dk_rope, cosine, sine_tab)
    latent_grad = line_share(jnp.concatenate([main_grad, rope_grad], axis=-1)).astype(jnp.bfloat16)
    query_rows_grad = weight_grads(
        normed, jnp.concatenate([query_grad, latent_grad], axis=1), places
    )
    normed_part = jnp.dot(query_grad, query_w, preferred_element_type=jnp.float32) + jnp.dot(
        latent_grad, down_w, preferred_element_type=jnp.float32
    )
    weighted_part = normed_part * inputs_full
    norm_gain_part = jnp.sum(weighted_part * scale_one, axis=0)
    stat_one = line_total(jnp.sum(weighted_part * norm_gain, axis=1))[:, None] / model_width
    moe_gain_part = jnp.where(mp_place == 0, moe_gain_part, 0.0)
    gain_total = small_total(
        jnp.concatenate([norm_gain_part, moe_gain_part, latent_gain_part]).reshape(-1, 128), 2
    ).reshape(-1)
    norm_gain_grad = gain_total[:model_width]
    moe_gain_grad = gain_total[model_width : 2 * model_width]
    latent_gain_grad = gain_total[2 * model_width :]
    normed_grad = mp_share(normed_part)
    input_grad = (
        residual_grad + scale_one * gain_one * normed_grad - inputs * scale_one**3 * stat_one
    )
    query_width = query_grad.shape[1]
    query_rows_grad, down_rows_grad = (
        query_rows_grad[:, :query_width].T,
        query_rows_grad[:, query_width:].T,
    )
    parts = [query_rows_grad[:nope_width].reshape(heads_here, DN, -1)]
    for half in range(2):
        low = nope_width + half * rope_width // 2
        parts.append(
            query_rows_grad[low : low + rope_width // 2].reshape(heads_here, DR // 2, -1)
        )
    query_weight_grad = jnp.concatenate(parts, axis=1).reshape(query_width, -1)
    latent_down_grad = down_rows_grad
    latent_up_grad = up_w_grad.T
    output_weight_grad = out_w_grad.T
    shared_gate_grad = moe_rows_grad[:, :hidden_here].T
    shared_up_grad = moe_rows_grad[:, hidden_here : 2 * hidden_here].T
    router_grad = moe_rows_grad[:, 2 * hidden_here :].T
    shared_down_grad = sdown_grad.T
    return (
        block_output,
        input_grad,
        norm_gain_grad,
        query_weight_grad,
        latent_down_grad,
        latent_gain_grad,
        latent_up_grad,
        output_weight_grad,
        moe_gain_grad,
        router_grad,
        shared_gate_grad,
        shared_up_grad,
        shared_down_grad,
        expert_gate_grad,
        expert_up_grad,
        expert_down_grad,
    )


def solution(mesh):
    in_specs = (
        P("dp", "mp"),
        P("dp", None),
        P("dp", None),
        P(),
        P("mp", "dp"),
        P("mp", "dp"),
        P(),
        P("mp", "dp"),
        P("mp", "dp"),
        P(),
        P(None, "dp"),
        P("mp", "dp"),
        P("mp", "dp"),
        P("mp", "dp"),
        P(("dp", "mp"), None, None),
        P(("dp", "mp"), None, None),
        P(("dp", "mp"), None, None),
        P("dp", "mp"),
    )
    out_specs = (
        P("dp", "mp"),
        P("dp", "mp"),
        P(),
        P("mp", "dp"),
        P("mp", "dp"),
        P(),
        P("mp", "dp"),
        P("mp", "dp"),
        P(),
        P(None, "dp"),
        P("mp", "dp"),
        P("mp", "dp"),
        P("mp", "dp"),
        P(("dp", "mp"), None, None),
        P(("dp", "mp"), None, None),
        P(("dp", "mp"), None, None),
    )

    return jax.shard_map(shards, mesh=mesh, in_specs=in_specs, out_specs=out_specs, check_vma=False)
```

profile of v0, /device:TPU:0, one launch (start us, length us, event | category | flops | bytes accessed | tf_op | source)
XLA Modules:
  0.0 928.5 jit_solution(12387215183425624068)
XLA Ops:
  10.5 50.3 %gather_all.1 = (bf16[512,2048]{1,0:T(8,128)(2,1)}, bf16[768,2048]{1,0:T(8,128)(2,1)}, bf16[144,2048]{1,0:T(8,128)(2,1)}, bf16[512,1024]{1,0:T(8,128)(2,1)}, bf1...) custom-call(bf16[512,512]{1,0:T(8,128)(2,1)} %refs_0_.1, bf16[768,256]{1,0:T(8,128)(2,1)} %pad_maximum_fusion.12.refs_1_, ...), custom_call_target="tpu_custom_call" | custom-call | bytes 144703488 | tf_op jit(solution)/shard_map/gather_all/pallas_call | solution.py:584
  66.1 16.4 %all_gather.12 = bf16[512,576]{0,1:T(8,128)(2,1)S(1)} all-gather(bf16[512,144]{0,1:T(8,128)(2,1)S(1)} %convolution_convert_fusion.16), channel_id=1, replica_groups=mesh['dp'=8,'mp'=4] {'mp'}, dimensions={1}, use_global_device_ids=true | all-gather | bytes 737280 | tf_op jit(solution)/shard_map/all_gather | solution.py:344
  121.5 20.2 %collective-permute-done.1.refs_2_ = bf16[2112,256]{1,0:T(8,128)(2,1)S(1)} collective-permute-done((bf16[2112,256]{1,0:T(8,128)(2,1)S(1)}, bf16[2112,256]{1,0:T(8,128)(2,1)S(1)}, u32[]{:S(2)}, u32[]{:S(2)}) %collective-permute-start.1) | collective-permute-done | bytes 1081376 | tf_op jit(solution)/shard_map/ppermute | solution.py:680
  144.1 15.4 %reduce-scatter.5.cloned.1.call-done = bf16[512,512]{1,0:T(8,128)(2,1)} async-done(((bf16[512,2048]{1,0:T(8,128)(2,1)}), bf16[512,512]{1,0:T(8,128)(2,1)}) %reduce-scatter.5.cloned.1.call-update) | async-done | bytes 524304 | tf_op jit(solution)/shard_map/reduce_scatter | solution.py:348
  205.1 8.6 assemble.1
  225.5 27.1 %all-gather.4.cloned.1.call-done = bf16[512,2048]{1,0:T(8,128)(2,1)} async-done(((bf16[512,512]{1,0:T(8,128)(2,1)}), bf16[512,2048]{1,0:T(8,128)(2,1)}) %all-gather.4.cloned.1.call-update) | async-done | bytes 2097168 | tf_op jit(solution)/shard_map/all_gather | solution.py:344
  270.5 10.5 %collective-permute-done.12.refs_4_ = bf16[256,2048]{1,0:T(8,128)(2,1)} collective-permute-done((bf16[256,2048]{1,0:T(8,128)(2,1)}, bf16[256,2048]{1,0:T(8,128)(2,1)}, u32[]{:S(2)}, u32[]{:S(2)}) %collective-permute-start.12) | collective-permute-done | bytes 1048608 | tf_op jit(solution)/shard_map/ppermute | solution.py:680
  298.5 12.5 %collective-permute-done.18.refs_0_ = bf16[256,2048]{1,0:T(8,128)(2,1)} collective-permute-done((bf16[256,2048]{1,0:T(8,128)(2,1)S(1)}, bf16[256,2048]{1,0:T(8,128)(2,1)}, u32[]{:S(2)}, u32[]{:S(2)}) %collective-permute-start.18) | collective-permute-done | bytes 1048608 | tf_op jit(solution)/shard_map/ppermute | solution.py:680
  312.6 20.9 %collective-permute-done.32.refs_1_ = bf16[256,2048]{1,0:T(8,128)(2,1)} collective-permute-done((bf16[256,2048]{1,0:T(8,128)(2,1)S(1)}, bf16[256,2048]{1,0:T(8,128)(2,1)}, u32[]{:S(2)}, u32[]{:S(2)}) %collective-permute-start.32) | collective-permute-done | bytes 1048608 | tf_op jit(solution)/shard_map/ppermute | solution.py:680
  335.2 30.8 %expert_rows.4 = (bf16[512,2048]{1,0:T(8,128)(2,1)}, bf16[512,2048]{1,0:T(8,128)(2,1)}, f32[1,1024]{1,0:T(1,128)}, bf16[704,4096]{1,0:T(8,128)(2,1)}, bf16[704,4...) custom-call(bf16[256,2048]{1,0:T(8,128)(2,1)} %copy-done.46, ...), custom_call_target="tpu_custom_call" | custom-call | flops 14763950080 | bytes 29622272 | tf_op jit(solution)/shard_map/expert_rows/pallas_call | solution.py:295
  368.7 30.8 %expert_rows.5 = (bf16[512,2048]{1,0:T(8,128)(2,1)}, bf16[512,2048]{1,0:T(8,128)(2,1)}, f32[1,1024]{1,0:T(1,128)}, bf16[704,4096]{1,0:T(8,128)(2,1)}, bf16[704,4...) custom-call(bf16[256,2048]{1,0:T(8,128)(2,1)} %collective-permute-do, ...), custom_call_target="tpu_custom_call", output_to_operand_aliasing={{3}: (13, {}), {4}: (14, {}), {5}: (15, {}), {6}: (16, {}),... | custom-call | flops 14763950080 | bytes 29622272 | tf_op jit(solution)/shard_map/expert_rows/pallas_call | solution.py:295
  400.8 31.0 %expert_rows.6 = (bf16[512,2048]{1,0:T(8,128)(2,1)}, bf16[512,2048]{1,0:T(8,128)(2,1)}, f32[1,1024]{1,0:T(1,128)}, bf16[704,4096]{1,0:T(8,128)(2,1)}, bf16[704,4...) custom-call(bf16[256,2048]{1,0:T(8,128)(2,1)} %collective-permute-do, ...), custom_call_target="tpu_custom_call", output_to_operand_aliasing={{3}: (13, {}), {4}: (14, {}), {5}: (15, {}), {6}: (16, {}),... | custom-call | flops 14763950080 | bytes 29622272 | tf_op jit(solution)/shard_map/expert_rows/pallas_call | solution.py:295
  433.3 31.1 %expert_rows.7 = (bf16[512,2048]{1,0:T(8,128)(2,1)}, bf16[512,2048]{1,0:T(8,128)(2,1)}, f32[1,1024]{1,0:T(1,128)}, bf16[704,4096]{1,0:T(8,128)(2,1)}, bf16[704,4...) custom-call(bf16[256,2048]{1,0:T(8,128)(2,1)} %collective-permute-do, ...), custom_call_target="tpu_custom_call", output_to_operand_aliasing={{3}: (13, {}), {4}: (14, {}), {5}: (15, {}), {6}: (16, {}),... | custom-call | flops 14763950080 | bytes 29622272 | tf_op jit(solution)/shard_map/expert_rows/pallas_call | solution.py:295
  464.9 29.7 %convolution_bitcast_fusion = f32[1,704,2048]{2,1,0:T(8,128)} fusion(bf16[704,4096]{1,0:T(8,128)(2,1)} %get-tuple-element.115, bf16[4096,2048]{1,0:T(8,128)(2,1)} %get-tuple-element.139), kind=kOutput, calls=%fused_computation.34 | convolution fusion | flops 11811160064 | bytes 28311552 | tf_op jit(solution)/shard_map/dot_general | solution.py:983
  501.3 21.2 %collective-permute-done.47 = bf16[256,2048]{1,0:T(8,128)(2,1)S(1)} collective-permute-done((bf16[256,2048]{1,0:T(8,128)(2,1)S(1)}, bf16[256,2048]{1,0:T(8,128)(2,1)S(1)}, u32[]{:S(2)}, u32[]{:S(2)}) %collective-permute-start.47) | collective-permute-done | bytes 1048608 | tf_op jit(solution)/shard_map/ppermute | solution.py:680
  528.5 13.9 %convolution_bitcast_fusion.1 = f32[1,704,2048]{2,1,0:T(8,128)} fusion(bf16[704,4096]{1,0:T(8,128)(2,1)S(1)} %bitcast.130, bf16[4096,2048]{1,0:T(8,128)(2,1)S(1)} %bitcast.128), kind=kOutput, calls=%fused_computation.35 | convolution fusion | flops 11811160064 | bytes 28311552 | tf_op jit(solution)/shard_map/dot_general | solution.py:987
  542.3 29.2 %collective-permute-done.48 = bf16[512,2048]{1,0:T(8,128)(2,1)} collective-permute-done((bf16[512,2048]{1,0:T(8,128)(2,1)}, bf16[512,2048]{1,0:T(8,128)(2,1)}, u32[]{:S(2)}, u32[]{:S(2)}) %collective-permute-start.48) | collective-permute-done | bytes 2097184 | tf_op jit(solution)/shard_map/ppermute | solution.py:680
  648.1 8.7 collective-permute-done.106
  670.7 17.0 %collective-permute-done.55 = bf16[256,2048]{1,0:T(8,128)(2,1)S(1)} collective-permute-done((bf16[256,2048]{1,0:T(8,128)(2,1)S(1)}, bf16[256,2048]{1,0:T(8,128)(2,1)S(1)}, u32[]{:S(2)}, u32[]{:S(2)}) %collective-permute-start.55) | collective-permute-done | bytes 1048608 | tf_op jit(solution)/shard_map/ppermute | solution.py:680
  702.8 19.2 %convolution_bitcast_fusion.2 = f32[1,704,2048]{2,1,0:T(8,128)} fusion(bf16[704,4096]{1,0:T(8,128)(2,1)} %get-tuple-element.136, bf16[4096,2048]{1,0:T(8,128)(2,1)} %get-tuple-element.137), kind=kOutput, calls=%fused_computation.36 | convolution fusion | flops 11811160064 | bytes 28311552 | tf_op jit(solution)/shard_map/dot_general | solution.py:984
  731.6 28.9 %collective-permute-done.56 = bf16[512,2048]{1,0:T(8,128)(2,1)S(1)} collective-permute-done((bf16[512,2048]{1,0:T(8,128)(2,1)}, bf16[512,2048]{1,0:T(8,128)(2,1)S(1)}, u32[]{:S(2)}, u32[]{:S(2)}) %collective-permute-start.56) | collective-permute-done | bytes 2097184 | tf_op jit(solution)/shard_map/ppermute | solution.py:680
  775.2 8.7 attend_backward.1
  812.4 10.2 %collective-permute-done.71 = bf16[512,144]{1,0:T(8,128)(2,1)S(1)} collective-permute-done((bf16[512,144]{1,0:T(8,128)(2,1)S(1)}, bf16[512,144]{1,0:T(8,128)(2,1)S(1)}, u32[]{:S(2)}, u32[]{:S(2)}) %collective-permute-start.71) | collective-permute-done | bytes 147488 | tf_op jit(solution)/shard_map/ppermute | solution.py:807
  835.3 11.2 %small_total.1 = f32[36,128]{1,0:T(8,128)} custom-call(f32[36,128]{1,0:T(8,128)} %maximum_bitcast_fusion.4.value_ref), custom_call_target="tpu_custom_call" | custom-call | bytes 4194304 | tf_op jit(solution)/shard_map/small_total/pallas_call | solution.py:652
  (686 shorter events, 401.6 us)
Async XLA Ops:
  7.2 152.3 %reduce-scatter.5.cloned.1.call-start = ((), (), s32[]{:S(2)}) async-start(), calls=%async_computation.4 | async-start | bytes 2621440 | tf_op jit(solution)/shard_map/reduce_scatter | solution.py:348
  117.6 96.1 %all-gather.6.cloned.1.call-start = ((), (), s32[]{:S(2)}) async-start(), calls=%async_computation.6 | async-start | bytes 2621440 | tf_op jit(solution)/shard_map/all_gather | solution.py:344
  118.3 134.3 %all-gather.4.cloned.1.call-start = ((), (), s32[]{:S(2)}) async-start(), calls=%async_computation.5 | async-start | bytes 2621440 | tf_op jit(solution)/shard_map/all_gather | solution.py:344
  120.9 84.1 %collective-permute-start = (bf16[2112,256]{1,0:T(8,128)(2,1)S(1)}, bf16[2112,256]{1,0:T(8,128)(2,1)}, u32[]{:S(2)}, u32[]{:S(2)}) collective-permute-start(bf16[2112,256]{1,0:T(8,128)(2,1)S(1)} %pad_maximum_fusion.6.refs_0_), channel_id=1, source_target_pairs={{0,4},{4,0},{8,12},{12,8},{16,20},{20,16},{24,28},{28,24},{1,5},{5... | collective-permute-start | bytes 3244040 | tf_op jit(solution)/shard_map/ppermute | solution.py:684
  120.9 64.1 %collective-permute-start.43 = (f32[512,16]{0,1:T(8,128)S(1)}, f32[512,16]{0,1:T(8,128)S(1)}, u32[]{:S(2)}, u32[]{:S(2)}) collective-permute-start(f32[512,16]{0,1:T(8,128)S(1)} %convert_reduce_fusion), channel_id=1, source_target_pairs={{0,4},{4,0},{8,12},{12,8},{16,20},{20,16},{24,28},{28,24},{1,5},{5... | collective-permute-start | bytes 98312 | tf_op jit(solution)/shard_map/ppermute | solution.py:684
  161.5 534.7 %reduce-scatter.9.cloned.1.call-start = ((), (), s32[]{:S(2)}) async-start(), calls=%async_computation.8 | async-start | bytes 2621440 | tf_op jit(solution)/shard_map/reduce_scatter | solution.py:348
  218.8 47.3 %collective-permute-start.35 = (bf16[256,2048]{1,0:T(8,128)(2,1)}, bf16[256,2048]{1,0:T(8,128)(2,1)}, u32[]{:S(2)}, u32[]{:S(2)}) collective-permute-start(bf16[256,2048]{1,0:T(8,128)(2,1)} %get-tuple-element.270.refs_5_), channel_id=1, source_target_pairs={{0,8},{4,12},{8,24},{12,28},{24,16},{28,20},{16,0},{20,4},{1,9},{5... | collective-permute-start | bytes 3145736 | tf_op jit(solution)/shard_map/ppermute | solution.py:680
  220.0 49.9 %collective-permute-start.13 = (bf16[256,2048]{1,0:T(8,128)(2,1)}, bf16[256,2048]{1,0:T(8,128)(2,1)S(1)}, u32[]{:S(2)}, u32[]{:S(2)}) collective-permute-start(bf16[256,2048]{1,0:T(8,128)(2,1)} %get-tuple-element.270.refs_5_), channel_id=1, source_target_pairs={{0,16},{4,20},{8,0},{12,4},{24,8},{28,12},{16,24},{20,28},{1,17},{... | collective-permute-start | bytes 3145736 | tf_op jit(solution)/shard_map/ppermute | solution.py:680
  282.5 50.9 %collective-permute-start.32 = (bf16[256,2048]{1,0:T(8,128)(2,1)S(1)}, bf16[256,2048]{1,0:T(8,128)(2,1)}, u32[]{:S(2)}, u32[]{:S(2)}) collective-permute-start(bf16[256,2048]{1,0:T(8,128)(2,1)S(1)} %get-tuple-element.272.refs_1_), channel_id=1, source_target_pairs={{0,8},{4,12},{8,24},{12,28},{24,16},{28,20},{16,0},{20,4},{1,9},{5... | collective-permute-start | bytes 3145736 | tf_op jit(solution)/shard_map/ppermute | solution.py:680
  297.0 69.0 %collective-permute-start.25 = (bf16[256,2048]{1,0:T(8,128)(2,1)S(1)}, bf16[256,2048]{1,0:T(8,128)(2,1)S(1)}, u32[]{:S(2)}, u32[]{:S(2)}) collective-permute-start(bf16[256,2048]{1,0:T(8,128)(2,1)S(1)} %collective-permute-done.13.refs_5_), channel_id=1, source_target_pairs={{0,16},{4,20},{8,0},{12,4},{24,8},{28,12},{16,24},{20,28},{1,17},{... | collective-permute-start | bytes 3145736 | tf_op jit(solution)/shard_map/ppermute | solution.py:680
  311.0 55.2 %collective-permute-start.33 = (bf16[256,2048]{1,0:T(8,128)(2,1)}, bf16[256,2048]{1,0:T(8,128)(2,1)}, u32[]{:S(2)}, u32[]{:S(2)}) collective-permute-start(bf16[256,2048]{1,0:T(8,128)(2,1)} %collective-permute-done.18.refs_0_), channel_id=1, source_target_pairs={{0,4},{4,0},{8,12},{12,8},{16,20},{20,16},{24,28},{28,24},{1,5},{5... | collective-permute-start | bytes 3145736 | tf_op jit(solution)/shard_map/ppermute | solution.py:684
  311.0 57.2 %collective-permute-start.19 = (bf16[256,2048]{1,0:T(8,128)(2,1)}, bf16[256,2048]{1,0:T(8,128)(2,1)}, u32[]{:S(2)}, u32[]{:S(2)}) collective-permute-start(bf16[256,2048]{1,0:T(8,128)(2,1)} %collective-permute-done.18.refs_0_), channel_id=1, source_target_pairs={{0,8},{4,12},{8,24},{12,28},{24,16},{28,20},{16,0},{20,4},{1,9},{5... | collective-permute-start | bytes 3145736 | tf_op jit(solution)/shard_map/ppermute | solution.py:680
  400.2 142.2 %collective-permute-start.44 = (bf16[512,2048]{1,0:T(8,128)(2,1)}, bf16[512,2048]{1,0:T(8,128)(2,1)}, u32[]{:S(2)}, u32[]{:S(2)}) collective-permute-start(bf16[512,2048]{1,0:T(8,128)(2,1)} %get-tuple-element.108), channel_id=1, source_target_pairs={{0,4},{4,0},{8,12},{12,8},{16,20},{20,16},{24,28},{28,24},{1,5},{5... | collective-permute-start | bytes 6291464 | tf_op jit(solution)/shard_map/ppermute | solution.py:684
  432.8 65.4 %collective-permute-start.45 = (bf16[512,2048]{1,0:T(8,128)(2,1)}, bf16[512,2048]{1,0:T(8,128)(2,1)S(1)}, u32[]{:S(2)}, u32[]{:S(2)}) collective-permute-start(bf16[512,2048]{1,0:T(8,128)(2,1)} %get-tuple-element.110), channel_id=1, source_target_pairs={{0,4},{4,0},{8,12},{12,8},{16,20},{20,16},{24,28},{28,24},{1,5},{5... | collective-permute-start | bytes 6291464 | tf_op jit(solution)/shard_map/ppermute | solution.py:684
  433.2 61.4 %collective-permute-start.46 = (bf16[512,2048]{1,0:T(8,128)(2,1)}, bf16[512,2048]{1,0:T(8,128)(2,1)}, u32[]{:S(2)}, u32[]{:S(2)}) collective-permute-start(bf16[512,2048]{1,0:T(8,128)(2,1)} %get-tuple-element.112), channel_id=1, source_target_pairs={{0,4},{4,0},{8,12},{12,8},{16,20},{20,16},{24,28},{28,24},{1,5},{5... | collective-permute-start | bytes 6291464 | tf_op jit(solution)/shard_map/ppermute | solution.py:684
  524.4 47.1 %collective-permute-start.48 = (bf16[512,2048]{1,0:T(8,128)(2,1)}, bf16[512,2048]{1,0:T(8,128)(2,1)}, u32[]{:S(2)}, u32[]{:S(2)}) collective-permute-start(bf16[512,2048]{1,0:T(8,128)(2,1)} %pad_maximum_fusion.1), channel_id=1, source_target_pairs={{0,16},{4,20},{8,0},{12,4},{24,8},{28,12},{16,24},{20,28},{1,17},{... | collective-permute-start | bytes 6291464 | tf_op jit(solution)/shard_map/ppermute | solution.py:680
  612.3 153.1 %all-gather.8.cloned.1.call-start = ((), (), s32[]{:S(2)}) async-start(), calls=%async_computation.9 | async-start | bytes 2621440 | tf_op jit(solution)/shard_map/all_gather | solution.py:344
  612.3 115.5 %collective-permute-start.52 = (bf16[512,2048]{1,0:T(8,128)(2,1)}, bf16[512,2048]{1,0:T(8,128)(2,1)}, u32[]{:S(2)}, u32[]{:S(2)}) collective-permute-start(bf16[512,2048]{1,0:T(8,128)(2,1)} %convolution_convert_fusion.10), channel_id=1, source_target_pairs={{0,4},{4,0},{8,12},{12,8},{16,20},{20,16},{24,28},{28,24},{1,5},{5... | collective-permute-start | bytes 6291464 | tf_op jit(solution)/shard_map/ppermute | solution.py:684
  698.5 219.6 %reduce-scatter.7.cloned.1.call-start = ((), (), s32[]{:S(2)}) async-start(), calls=%async_computation.7 | async-start | bytes 2621440 | tf_op jit(solution)/shard_map/reduce_scatter | solution.py:348
  700.6 59.9 %collective-permute-start.56 = (bf16[512,2048]{1,0:T(8,128)(2,1)}, bf16[512,2048]{1,0:T(8,128)(2,1)S(1)}, u32[]{:S(2)}, u32[]{:S(2)}) collective-permute-start(bf16[512,2048]{1,0:T(8,128)(2,1)} %pad_maximum_fusion.3), channel_id=1, source_target_pairs={{0,16},{4,20},{8,0},{12,4},{24,8},{28,12},{16,24},{20,28},{1,17},{... | collective-permute-start | bytes 6291464 | tf_op jit(solution)/shard_map/ppermute | solution.py:680
  701.6 59.7 %collective-permute-start.59 = (bf16[512,2048]{1,0:T(8,128)(2,1)}, bf16[512,2048]{1,0:T(8,128)(2,1)S(1)}, u32[]{:S(2)}, u32[]{:S(2)}) collective-permute-start(bf16[512,2048]{1,0:T(8,128)(2,1)} %pad_maximum_fusion.4), channel_id=1, source_target_pairs={{0,8},{4,12},{8,24},{12,28},{24,16},{28,20},{16,0},{20,4},{1,9},{5... | collective-permute-start | bytes 6291464 | tf_op jit(solution)/shard_map/ppermute | solution.py:680
  765.1 153.0 %reduce-scatter.11.cloned.1.call-start = ((), (), s32[]{:S(2)}) async-start(), calls=%async_computation.10 | async-start | bytes 2621440 | tf_op jit(solution)/shard_map/reduce_scatter | solution.py:348
  789.6 75.5 %collective-permute-start.93 = (bf16[256,512]{1,0:T(8,128)(2,1)}, bf16[256,512]{1,0:T(8,128)(2,1)}, u32[]{:S(2)}, u32[]{:S(2)}) collective-permute-start(bf16[256,512]{1,0:T(8,128)(2,1)} %get-tuple-element.262), channel_id=1, source_target_pairs={{0,4},{4,0},{8,12},{12,8},{16,20},{20,16},{24,28},{28,24},{1,5},{5... | collective-permute-start | bytes 786440 | tf_op jit(solution)/shard_map/ppermute | solution.py:684
  789.6 76.1 %collective-permute-start.94 = (bf16[256,512]{1,0:T(8,128)(2,1)}, bf16[256,512]{1,0:T(8,128)(2,1)}, u32[]{:S(2)}, u32[]{:S(2)}) collective-permute-start(bf16[256,512]{1,0:T(8,128)(2,1)} %get-tuple-element.261), channel_id=1, source_target_pairs={{0,4},{4,0},{8,12},{12,8},{16,20},{20,16},{24,28},{28,24},{1,5},{5... | collective-permute-start | bytes 786440 | tf_op jit(solution)/shard_map/ppermute | solution.py:684
  (229 other events, 3608.1 us)
Sparse Core Ops, SparseCore 0:
  117.7 41.7 reduce-scatter.4
  161.1 44.8 all-gather.5
  208.1 44.4 all-gather.3
  612.4 41.0 reduce-scatter.8
  698.6 43.2 all-gather.7
  765.2 41.4 reduce-scatter.6
  855.8 42.9 reduce-scatter.10
where the time goes:
time: 938 us; the launch traced here: 929 us
  waiting for transfers between devices  306 us (33%)
  Pallas kernels  209 us (22%)
  matrix products  156 us (17%)
  starting transfers between devices  90.4 us (10%)
  other arithmetic  75.5 us (8%)
  local copies, waits for them, and re-layouts  52.5 us (6%)
  between operations  23.3 us (2%)
  blocking collectives  16.4 us (2%)
    ppermute x48, waiting for transfers between devices, ring_move(): return lax.ppermute(values, 'dp', pairs)  246 us
    pallas_call x4, Pallas kernels, expert_rows(): pl.pallas_call(functools.partial(expert_kernel, len(held)), grid=(2,), ou...  124 us
    ppermute x48, starting transfers between devices, ring_move(): return lax.ppermute(values, 'dp', pairs)  54.8 us
    pallas_call x1, Pallas kernels, gather_all(): pl.pallas_call(functools.partial(gather_kernel, dp_count, mp_count, tuple...  50.3 us
    dot_general x8, matrix products, out_rows(): jnp.dot(act_late[:, low:low + tokens_here].T, own_down, preferred_element...  30.2 us
    dot_general x1, matrix products, shards(): jnp.dot(act_all, grads_all, preferred_element_type=jnp.float32)[None]  29.7 us
    all_gather x3, waiting for transfers between devices, full_rows(): return lax.all_gather(piece_rows, 'mp', axis=1, tiled=True)  27.2 us
    dot_general x1, matrix products, shards(): jnp.dot(gate_pre_all, rows_all, preferred_element_type=jnp.float32)[None]  19.2 us
  transfers between devices with their start and end apart: 123, of which 37 were waited for; matrix products, arithmetic and copies ran while one was open for 24% of the time, Pallas kernels for 16%

commit v1 on v0

--- a/solution.py
+++ b/solution.py
@@ -199,46 +199,74 @@
     )(probs, grad, q_nope, q_rope, keys_values, k_rope)
 
 
-def expert_kernel(held, *refs):
+def expert_kernel(held, k, *refs):
     xs, gs = refs[:4], refs[4:8]
     mask_ref, own_ref, *weights = refs[8:13]
     refs = refs[13 + held :]
     back_same, back_other, score_ref, act_ref, gate_pre_ref, up_pre_ref, x_all, g_all = refs[:8]
-    pre_gate, pre_up, grads, gate_ref, up_ref, down_ref, arrived = refs[8:]
+    x_kept, g_kept, pre_gate, pre_up, grads, gate_ref, up_ref, down_ref = refs[8:16]
+    arrived, landed, stored = refs[16:]
     hidden = gate_ref.shape[0]
+    half, tokens = xs[0].shape[0], 2 * xs[0].shape[0]
     nt = (((1,), (1,)), ((), ()))
     tn = (((0,), (0,)), ((), ()))
-    first = pl.program_id(0) == 0
-    copies = [
+    slot = pl.program_id(0)
+    first = slot == 0
+    into = [
         pltpu.make_async_copy(weight, kept, arrived.at[i])
         for i, (weight, kept) in enumerate(zip(weights, (gate_ref, up_ref, down_ref)))
     ]
 
+    def take(sources, kept, i, part):
+        return pltpu.make_async_copy(
+            sources[part],
+            kept.at[part // 2, pl.ds(part % 2 * half, half), :],
+            landed.at[i, part],
+        )
+
+    def store(kept, whole, i, part):
+        rows = pl.ds((2 * k + part) * tokens, tokens)
+        return pltpu.make_async_copy(kept.at[part], whole.at[rows, :], stored.at[i, part])
+
     @pl.when(first)
     def _():
-        for copy in copies:
+        for part in range(2):
+            take(xs, x_kept, 0, part).start()
+        for copy in into:
             copy.start()
-
-    half = xs[0].shape[0]
-    for part in range(2):
-        rows = slice(part * half, (part + 1) * half)
-        x_all[rows, :] = jnp.where(first, xs[part][...], xs[part + 2][...])
-        g_all[rows, :] = jnp.where(first, gs[part][...], gs[part + 2][...])
-
-    def arrive(i):
+        for part in range(2):
+            take(gs, g_kept, 1, part).start()
+        for part in range(2, 4):
+            take(xs, x_kept, 0, part).start()
+            take(gs, g_kept, 1, part).start()
+
+    def arrive(sources, kept, whole, i):
+        for core in range(2):
+
+            @pl.when(slot == core)
+            def _(core=core):
+                take(sources, kept, i, 2 * core).wait()
+                take(sources, kept, i, 2 * core + 1).wait()
+                store(kept, whole, i, core).start()
+
+    def arrive_weight(i):
         @pl.when(first)
         def _():
-            copies[i].wait()
-
-    arrive(0)
+            into[i].wait()
+
+    arrive(xs, x_kept, x_all, 0)
+    arrive_weight(0)
     pre_gate[...] = lax.dot_general(
-        gate_ref[...], x_all[...], nt, preferred_element_type=jnp.float32
-    )
-    arrive(1)
-    pre_up[...] = lax.dot_general(up_ref[...], x_all[...], nt, preferred_element_type=jnp.float32)
-    arrive(2)
+        gate_ref[...], x_kept[slot], nt, preferred_element_type=jnp.float32
+    )
+    arrive_weight(1)
+    pre_up[...] = lax.dot_general(
+        up_ref[...], x_kept[slot], nt, preferred_element_type=jnp.float32
+    )
+    arrive(gs, g_kept, g_all, 1)
+    arrive_weight(2)
     grads[...] = lax.dot_general(
-        down_ref[...], g_all[...], nt, preferred_element_type=jnp.float32
+        down_ref[...], g_kept[slot], nt, preferred_element_type=jnp.float32
     )
     mask = mask_ref[...]
     pick_exp = jnp.exp(jnp.where(mask > 0, pre_up[hidden:, :], negative))
@@ -262,7 +290,7 @@
         return score + jnp.sum(activation * grad, axis=0, keepdims=True)
 
     score_ref[...] = lax.fori_loop(
-        0, hidden // step, body, jnp.zeros((1, x_all.shape[0]), jnp.float32)
+        0, hidden // step, body, jnp.zeros((1, tokens), jnp.float32)
     )
     width = 512
     for low in range(0, gate_ref.shape[1], width):
@@ -281,6 +309,12 @@
         @pl.when(jnp.logical_not(first))
         def _(back=back, columns=columns):
             back_other[:, columns] = back
+
+    @pl.when(jnp.logical_not(first))
+    def _():
+        for part in range(2):
+            store(x_kept, x_all, 0, part).wait()
+            store(g_kept, g_all, 1, part).wait()
 
 
 def expert_rows(k, chips, rows, grads, mask, own, gate, up_router, down, held):
@@ -291,9 +325,9 @@
     bf = jnp.bfloat16
     total = 2 * chips * tokens
     slab = pl.BlockSpec((hidden, tokens), lambda i: (0, 2 * k + i))
-    lines = pl.BlockSpec((tokens, width), lambda i: (2 * k + i, 0))
+    anywhere = pl.BlockSpec(memory_space=pl.ANY)
     return pl.pallas_call(
-        functools.partial(expert_kernel, len(held)),
+        functools.partial(expert_kernel, len(held), k),
         grid=(2,),
         out_shape=(
             jax.ShapeDtypeStruct((tokens, width), bf),
@@ -306,10 +340,10 @@
             jax.ShapeDtypeStruct((total, width), bf),
         ),
         in_specs=[
-            *[whole((half, width))] * 8,
+            *[anywhere] * 8,
             pl.BlockSpec((mask.shape[0], tokens), lambda i: (0, i)),
             whole(own.shape),
-            *[pl.BlockSpec(memory_space=pl.ANY)] * (3 + len(held)),
+            *[anywhere] * (3 + len(held)),
         ],
         out_specs=(
             whole((tokens, width)),
@@ -318,10 +352,12 @@
             slab,
             slab,
             slab,
-            lines,
-            lines,
+            anywhere,
+            anywhere,
         ),
         scratch_shapes=[
+            pltpu.VMEM((2, tokens, width), bf),
+            pltpu.VMEM((2, tokens, width), bf),
             pltpu.VMEM((hidden, tokens), jnp.float32),
             pltpu.VMEM((up_router.shape[0], tokens), jnp.float32),
             pltpu.VMEM((hidden, tokens), jnp.float32),
@@ -329,6 +365,8 @@
             pltpu.VMEM(up_router.shape, bf),
             pltpu.VMEM(down.shape, bf),
             pltpu.SemaphoreType.DMA((3,)),
+            pltpu.SemaphoreType.DMA((2, 4)),
+            pltpu.SemaphoreType.DMA((2, 2)),
         ],
         input_output_aliases={13 + i: 3 + i for i in range(len(held))},
         cost_estimate=pl.CostEstimate(

time: 938 us -> 930 us (level)
  matrix products: 156 us -> 145 us
  starting transfers between devices: 90.4 us -> 101 us
    ppermute x48, starting transfers between devices: 54.8 us -> 65.6 us  [ring_move(): return lax.ppermute(values, 'dp', pairs)]
    dot_general x1, matrix products: 29.7 us -> 19 us  [shards(): jnp.dot(act_all, grads_all, preferred_element_type=jnp.float32)[None]]
  transfers between devices with their start and end apart: 123 -> 123, of which waited for: 37 -> 37; matrix products, arithmetic and copies ran while one was open for 24% -> 23% of each run, Pallas kernels for 16% -> 16%
where the time goes in v1:
time: 930 us; the launch traced here: 920 us
  waiting for transfers between devices  306 us (33%)
  Pallas kernels  201 us (22%)
  matrix products  145 us (16%)
  starting transfers between devices  101 us (11%)
  other arithmetic  75.5 us (8%)
  local copies, waits for them, and re-layouts  52 us (6%)
  between operations  23.3 us (3%)
  blocking collectives  16.4 us (2%)
    ppermute x48, waiting for transfers between devices, ring_move(): return lax.ppermute(values, 'dp', pairs)  246 us
    pallas_call x4, Pallas kernels, expert_rows(): pl.pallas_call(functools.partial(expert_kernel, len(held), k), grid=(2,),...  116 us
    ppermute x48, starting transfers between devices, ring_move(): return lax.ppermute(values, 'dp', pairs)  65.6 us
    pallas_call x1, Pallas kernels, gather_all(): pl.pallas_call(functools.partial(gather_kernel, dp_count, mp_count, tuple...  50.3 us
    dot_general x8, matrix products, out_rows(): jnp.dot(act_late[:, low:low + tokens_here].T, own_down, preferred_element...  30.2 us
    all_gather x3, waiting for transfers between devices, full_rows(): return lax.all_gather(piece_rows, 'mp', axis=1, tiled=True)  27.2 us
    dot_general x1, matrix products, shards(): jnp.dot(gate_pre_all, rows_all, preferred_element_type=jnp.float32)[None]  19.2 us
    dot_general x1, matrix products, shards(): jnp.dot(act_all, grads_all, preferred_element_type=jnp.float32)[None]  19 us
  transfers between devices with their start and end apart: 123, of which 37 were waited for; matrix products, arithmetic and copies ran while one was open for 23% of the time, Pallas kernels for 16%

profile of v1, /device:TPU:0, one launch (start us, length us, event | category | flops | bytes accessed | tf_op | source)
XLA Modules:
  0.0 920.0 jit_solution(13970979338603656241)
XLA Ops:
  10.5 50.3 %gather_all.1 = (bf16[512,2048]{1,0:T(8,128)(2,1)}, bf16[768,2048]{1,0:T(8,128)(2,1)}, bf16[144,2048]{1,0:T(8,128)(2,1)}, bf16[512,1024]{1,0:T(8,128)(2,1)}, bf1...) custom-call(bf16[512,512]{1,0:T(8,128)(2,1)} %refs_0_.1, bf16[768,256]{1,0:T(8,128)(2,1)} %pad_maximum_fusion.12.refs_1_, ...), custom_call_target="tpu_custom_call" | custom-call | bytes 144703488 | tf_op jit(solution)/shard_map/gather_all/pallas_call | solution.py:622
  66.1 16.4 %all_gather.12 = bf16[512,576]{0,1:T(8,128)(2,1)S(1)} all-gather(bf16[512,144]{0,1:T(8,128)(2,1)S(1)} %convolution_convert_fusion.16), channel_id=1, replica_groups=mesh['dp'=8,'mp'=4] {'mp'}, dimensions={1}, use_global_device_ids=true | all-gather | bytes 737280 | tf_op jit(solution)/shard_map/all_gather | solution.py:382
  121.5 20.2 %collective-permute-done.1.refs_2_ = bf16[2112,256]{1,0:T(8,128)(2,1)S(1)} collective-permute-done((bf16[2112,256]{1,0:T(8,128)(2,1)S(1)}, bf16[2112,256]{1,0:T(8,128)(2,1)S(1)}, u32[]{:S(2)}, u32[]{:S(2)}) %collective-permute-start.1) | collective-permute-done | bytes 1081376 | tf_op jit(solution)/shard_map/ppermute | solution.py:718
  144.1 15.4 %reduce-scatter.5.cloned.1.call-done = bf16[512,512]{1,0:T(8,128)(2,1)} async-done(((bf16[512,2048]{1,0:T(8,128)(2,1)}), bf16[512,512]{1,0:T(8,128)(2,1)}) %reduce-scatter.5.cloned.1.call-update) | async-done | bytes 524304 | tf_op jit(solution)/shard_map/reduce_scatter | solution.py:386
  225.5 27.1 %all-gather.4.cloned.1.call-done = bf16[512,2048]{1,0:T(8,128)(2,1)} async-done(((bf16[512,512]{1,0:T(8,128)(2,1)}), bf16[512,2048]{1,0:T(8,128)(2,1)}) %all-gather.4.cloned.1.call-update) | async-done | bytes 2097168 | tf_op jit(solution)/shard_map/all_gather | solution.py:382
  270.5 10.5 %collective-permute-done.12.refs_4_ = bf16[256,2048]{1,0:T(8,128)(2,1)} collective-permute-done((bf16[256,2048]{1,0:T(8,128)(2,1)}, bf16[256,2048]{1,0:T(8,128)(2,1)}, u32[]{:S(2)}, u32[]{:S(2)}) %collective-permute-start.12) | collective-permute-done | bytes 1048608 | tf_op jit(solution)/shard_map/ppermute | solution.py:718
  298.5 12.5 %collective-permute-done.18.refs_0_ = bf16[256,2048]{1,0:T(8,128)(2,1)} collective-permute-done((bf16[256,2048]{1,0:T(8,128)(2,1)S(1)}, bf16[256,2048]{1,0:T(8,128)(2,1)}, u32[]{:S(2)}, u32[]{:S(2)}) %collective-permute-start.18) | collective-permute-done | bytes 1048608 | tf_op jit(solution)/shard_map/ppermute | solution.py:718
  312.6 20.9 %collective-permute-done.32.refs_1_ = bf16[256,2048]{1,0:T(8,128)(2,1)} collective-permute-done((bf16[256,2048]{1,0:T(8,128)(2,1)S(1)}, bf16[256,2048]{1,0:T(8,128)(2,1)}, u32[]{:S(2)}, u32[]{:S(2)}) %collective-permute-start.32) | collective-permute-done | bytes 1048608 | tf_op jit(solution)/shard_map/ppermute | solution.py:718
  335.2 28.8 %expert_rows.4 = (bf16[512,2048]{1,0:T(8,128)(2,1)}, bf16[512,2048]{1,0:T(8,128)(2,1)}, f32[1,1024]{1,0:T(1,128)}, bf16[704,4096]{1,0:T(8,128)(2,1)}, bf16[704,4...) custom-call(bf16[256,2048]{1,0:T(8,128)(2,1)} %copy-done.46, ...), custom_call_target="tpu_custom_call" | custom-call | flops 14763950080 | bytes 29622272 | tf_op jit(solution)/shard_map/expert_rows/pallas_call | solution.py:329
  366.7 28.8 %expert_rows.5 = (bf16[512,2048]{1,0:T(8,128)(2,1)}, bf16[512,2048]{1,0:T(8,128)(2,1)}, f32[1,1024]{1,0:T(1,128)}, bf16[704,4096]{1,0:T(8,128)(2,1)}, bf16[704,4...) custom-call(bf16[256,2048]{1,0:T(8,128)(2,1)} %collective-permute-do, ...), custom_call_target="tpu_custom_call", output_to_operand_aliasing={{3}: (13, {}), {4}: (14, {}), {5}: (15, {}), {6}: (16, {}),... | custom-call | flops 14763950080 | bytes 29622272 | tf_op jit(solution)/shard_map/expert_rows/pallas_call | solution.py:329
  396.7 29.0 %expert_rows.6 = (bf16[512,2048]{1,0:T(8,128)(2,1)}, bf16[512,2048]{1,0:T(8,128)(2,1)}, f32[1,1024]{1,0:T(1,128)}, bf16[704,4096]{1,0:T(8,128)(2,1)}, bf16[704,4...) custom-call(bf16[256,2048]{1,0:T(8,128)(2,1)} %collective-permute-do, ...), custom_call_target="tpu_custom_call", output_to_operand_aliasing={{3}: (13, {}), {4}: (14, {}), {5}: (15, {}), {6}: (16, {}),... | custom-call | flops 14763950080 | bytes 29622272 | tf_op jit(solution)/shard_map/expert_rows/pallas_call | solution.py:329
  427.2 29.1 %expert_rows.7 = (bf16[512,2048]{1,0:T(8,128)(2,1)}, bf16[512,2048]{1,0:T(8,128)(2,1)}, f32[1,1024]{1,0:T(1,128)}, bf16[704,4096]{1,0:T(8,128)(2,1)}, bf16[704,4...) custom-call(bf16[256,2048]{1,0:T(8,128)(2,1)} %collective-permute-do, ...), custom_call_target="tpu_custom_call", output_to_operand_aliasing={{3}: (13, {}), {4}: (14, {}), {5}: (15, {}), {6}: (16, {}),... | custom-call | flops 14763950080 | bytes 29622272 | tf_op jit(solution)/shard_map/expert_rows/pallas_call | solution.py:329
  456.8 19.0 %convolution_bitcast_fusion = f32[1,704,2048]{2,1,0:T(8,128)} fusion(bf16[704,4096]{1,0:T(8,128)(2,1)} %get-tuple-element.115, bf16[4096,2048]{1,0:T(8,128)(2,1)} %get-tuple-element.139), kind=kOutput, calls=%fused_computation.34 | convolution fusion | flops 11811160064 | bytes 28311552 | tf_op jit(solution)/shard_map/dot_general | solution.py:1021
  478.4 11.3 %collective-permute-start.47 = (bf16[256,2048]{1,0:T(8,128)(2,1)S(1)}, bf16[256,2048]{1,0:T(8,128)(2,1)S(1)}, u32[]{:S(2)}, u32[]{:S(2)}) collective-permute-start(bf16[256,2048]{1,0:T(8,128)(2,1)S(1)} %get-tuple-element.268), channel_id=1, source_target_pairs={{0,16},{4,20},{8,0},{12,4},{24,8},{28,12},{16,24},{20,28},{1,17},{... | collective-permute-start | bytes 3145736 | tf_op jit(solution)/shard_map/ppermute | solution.py:718
  492.8 21.2 %collective-permute-done.47 = bf16[256,2048]{1,0:T(8,128)(2,1)S(1)} collective-permute-done((bf16[256,2048]{1,0:T(8,128)(2,1)S(1)}, bf16[256,2048]{1,0:T(8,128)(2,1)S(1)}, u32[]{:S(2)}, u32[]{:S(2)}) %collective-permute-start.47) | collective-permute-done | bytes 1048608 | tf_op jit(solution)/shard_map/ppermute | solution.py:718
  520.0 13.9 %convolution_bitcast_fusion.1 = f32[1,704,2048]{2,1,0:T(8,128)} fusion(bf16[704,4096]{1,0:T(8,128)(2,1)S(1)} %bitcast.130, bf16[4096,2048]{1,0:T(8,128)(2,1)S(1)} %bitcast.128), kind=kOutput, calls=%fused_computation.35 | convolution fusion | flops 11811160064 | bytes 28311552 | tf_op jit(solution)/shard_map/dot_general | solution.py:1025
  533.9 29.2 %collective-permute-done.48 = bf16[512,2048]{1,0:T(8,128)(2,1)} collective-permute-done((bf16[512,2048]{1,0:T(8,128)(2,1)}, bf16[512,2048]{1,0:T(8,128)(2,1)}, u32[]{:S(2)}, u32[]{:S(2)}) %collective-permute-start.48) | collective-permute-done | bytes 2097184 | tf_op jit(solution)/shard_map/ppermute | solution.py:718
  639.6 8.7 collective-permute-done.106
  662.2 17.0 %collective-permute-done.55 = bf16[256,2048]{1,0:T(8,128)(2,1)S(1)} collective-permute-done((bf16[256,2048]{1,0:T(8,128)(2,1)S(1)}, bf16[256,2048]{1,0:T(8,128)(2,1)S(1)}, u32[]{:S(2)}, u32[]{:S(2)}) %collective-permute-start.55) | collective-permute-done | bytes 1048608 | tf_op jit(solution)/shard_map/ppermute | solution.py:718
  694.3 19.2 %convolution_bitcast_fusion.2 = f32[1,704,2048]{2,1,0:T(8,128)} fusion(bf16[704,4096]{1,0:T(8,128)(2,1)} %get-tuple-element.136, bf16[4096,2048]{1,0:T(8,128)(2,1)} %get-tuple-element.137), kind=kOutput, calls=%fused_computation.36 | convolution fusion | flops 11811160064 | bytes 28311552 | tf_op jit(solution)/shard_map/dot_general | solution.py:1022
  723.2 28.9 %collective-permute-done.56 = bf16[512,2048]{1,0:T(8,128)(2,1)S(1)} collective-permute-done((bf16[512,2048]{1,0:T(8,128)(2,1)}, bf16[512,2048]{1,0:T(8,128)(2,1)S(1)}, u32[]{:S(2)}, u32[]{:S(2)}) %collective-permute-start.56) | collective-permute-done | bytes 2097184 | tf_op jit(solution)/shard_map/ppermute | solution.py:718
  766.8 8.7 attend_backward.1
  803.9 10.2 %collective-permute-done.71 = bf16[512,144]{1,0:T(8,128)(2,1)S(1)} collective-permute-done((bf16[512,144]{1,0:T(8,128)(2,1)S(1)}, bf16[512,144]{1,0:T(8,128)(2,1)S(1)}, u32[]{:S(2)}, u32[]{:S(2)}) %collective-permute-start.71) | collective-permute-done | bytes 147488 | tf_op jit(solution)/shard_map/ppermute | solution.py:845
  826.8 11.2 %small_total.1 = f32[36,128]{1,0:T(8,128)} custom-call(f32[36,128]{1,0:T(8,128)} %maximum_bitcast_fusion.4.value_ref), custom_call_target="tpu_custom_call" | custom-call | bytes 4194304 | tf_op jit(solution)/shard_map/small_total/pallas_call | solution.py:690
  (686 shorter events, 409.2 us)
Async XLA Ops:
  7.2 152.3 %reduce-scatter.5.cloned.1.call-start = ((), (), s32[]{:S(2)}) async-start(), calls=%async_computation.4 | async-start | bytes 2621440 | tf_op jit(solution)/shard_map/reduce_scatter | solution.py:386
  117.6 96.1 %all-gather.6.cloned.1.call-start = ((), (), s32[]{:S(2)}) async-start(), calls=%async_computation.6 | async-start | bytes 2621440 | tf_op jit(solution)/shard_map/all_gather | solution.py:382
  118.3 134.3 %all-gather.4.cloned.1.call-start = ((), (), s32[]{:S(2)}) async-start(), calls=%async_computation.5 | async-start | bytes 2621440 | tf_op jit(solution)/shard_map/all_gather | solution.py:382
  120.9 84.1 %collective-permute-start = (bf16[2112,256]{1,0:T(8,128)(2,1)S(1)}, bf16[2112,256]{1,0:T(8,128)(2,1)}, u32[]{:S(2)}, u32[]{:S(2)}) collective-permute-start(bf16[2112,256]{1,0:T(8,128)(2,1)S(1)} %pad_maximum_fusion.6.refs_0_), channel_id=1, source_target_pairs={{0,4},{4,0},{8,12},{12,8},{16,20},{20,16},{24,28},{28,24},{1,5},{5... | collective-permute-start | bytes 3244040 | tf_op jit(solution)/shard_map/ppermute | solution.py:722
  120.9 64.1 %collective-permute-start.43 = (f32[512,16]{0,1:T(8,128)S(1)}, f32[512,16]{0,1:T(8,128)S(1)}, u32[]{:S(2)}, u32[]{:S(2)}) collective-permute-start(f32[512,16]{0,1:T(8,128)S(1)} %convert_reduce_fusion), channel_id=1, source_target_pairs={{0,4},{4,0},{8,12},{12,8},{16,20},{20,16},{24,28},{28,24},{1,5},{5... | collective-permute-start | bytes 98312 | tf_op jit(solution)/shard_map/ppermute | solution.py:722
  161.5 526.2 %reduce-scatter.9.cloned.1.call-start = ((), (), s32[]{:S(2)}) async-start(), calls=%async_computation.8 | async-start | bytes 2621440 | tf_op jit(solution)/shard_map/reduce_scatter | solution.py:386
  218.8 47.3 %collective-permute-start.35 = (bf16[256,2048]{1,0:T(8,128)(2,1)}, bf16[256,2048]{1,0:T(8,128)(2,1)}, u32[]{:S(2)}, u32[]{:S(2)}) collective-permute-start(bf16[256,2048]{1,0:T(8,128)(2,1)} %get-tuple-element.270.refs_5_), channel_id=1, source_target_pairs={{0,8},{4,12},{8,24},{12,28},{24,16},{28,20},{16,0},{20,4},{1,9},{5... | collective-permute-start | bytes 3145736 | tf_op jit(solution)/shard_map/ppermute | solution.py:718
  220.0 49.9 %collective-permute-start.13 = (bf16[256,2048]{1,0:T(8,128)(2,1)}, bf16[256,2048]{1,0:T(8,128)(2,1)S(1)}, u32[]{:S(2)}, u32[]{:S(2)}) collective-permute-start(bf16[256,2048]{1,0:T(8,128)(2,1)} %get-tuple-element.270.refs_5_), channel_id=1, source_target_pairs={{0,16},{4,20},{8,0},{12,4},{24,8},{28,12},{16,24},{20,28},{1,17},{... | collective-permute-start | bytes 3145736 | tf_op jit(solution)/shard_map/ppermute | solution.py:718
  282.5 50.9 %collective-permute-start.32 = (bf16[256,2048]{1,0:T(8,128)(2,1)S(1)}, bf16[256,2048]{1,0:T(8,128)(2,1)}, u32[]{:S(2)}, u32[]{:S(2)}) collective-permute-start(bf16[256,2048]{1,0:T(8,128)(2,1)S(1)} %get-tuple-element.272.refs_1_), channel_id=1, source_target_pairs={{0,8},{4,12},{8,24},{12,28},{24,16},{28,20},{16,0},{20,4},{1,9},{5... | collective-permute-start | bytes 3145736 | tf_op jit(solution)/shard_map/ppermute | solution.py:718
  297.0 66.9 %collective-permute-start.25 = (bf16[256,2048]{1,0:T(8,128)(2,1)S(1)}, bf16[256,2048]{1,0:T(8,128)(2,1)S(1)}, u32[]{:S(2)}, u32[]{:S(2)}) collective-permute-start(bf16[256,2048]{1,0:T(8,128)(2,1)S(1)} %collective-permute-done.13.refs_5_), channel_id=1, source_target_pairs={{0,16},{4,20},{8,0},{12,4},{24,8},{28,12},{16,24},{20,28},{1,17},{... | collective-permute-start | bytes 3145736 | tf_op jit(solution)/shard_map/ppermute | solution.py:718
  311.0 53.2 %collective-permute-start.33 = (bf16[256,2048]{1,0:T(8,128)(2,1)}, bf16[256,2048]{1,0:T(8,128)(2,1)}, u32[]{:S(2)}, u32[]{:S(2)}) collective-permute-start(bf16[256,2048]{1,0:T(8,128)(2,1)} %collective-permute-done.18.refs_0_), channel_id=1, source_target_pairs={{0,4},{4,0},{8,12},{12,8},{16,20},{20,16},{24,28},{28,24},{1,5},{5... | collective-permute-start | bytes 3145736 | tf_op jit(solution)/shard_map/ppermute | solution.py:722
  311.0 55.2 %collective-permute-start.19 = (bf16[256,2048]{1,0:T(8,128)(2,1)}, bf16[256,2048]{1,0:T(8,128)(2,1)}, u32[]{:S(2)}, u32[]{:S(2)}) collective-permute-start(bf16[256,2048]{1,0:T(8,128)(2,1)} %collective-permute-done.18.refs_0_), channel_id=1, source_target_pairs={{0,8},{4,12},{8,24},{12,28},{24,16},{28,20},{16,0},{20,4},{1,9},{5... | collective-permute-start | bytes 3145736 | tf_op jit(solution)/shard_map/ppermute | solution.py:718
  396.1 137.8 %collective-permute-start.44 = (bf16[512,2048]{1,0:T(8,128)(2,1)}, bf16[512,2048]{1,0:T(8,128)(2,1)}, u32[]{:S(2)}, u32[]{:S(2)}) collective-permute-start(bf16[512,2048]{1,0:T(8,128)(2,1)} %get-tuple-element.108), channel_id=1, source_target_pairs={{0,4},{4,0},{8,12},{12,8},{16,20},{20,16},{24,28},{28,24},{1,5},{5... | collective-permute-start | bytes 6291464 | tf_op jit(solution)/shard_map/ppermute | solution.py:722
  426.7 63.0 %collective-permute-start.45 = (bf16[512,2048]{1,0:T(8,128)(2,1)}, bf16[512,2048]{1,0:T(8,128)(2,1)S(1)}, u32[]{:S(2)}, u32[]{:S(2)}) collective-permute-start(bf16[512,2048]{1,0:T(8,128)(2,1)} %get-tuple-element.110), channel_id=1, source_target_pairs={{0,4},{4,0},{8,12},{12,8},{16,20},{20,16},{24,28},{28,24},{1,5},{5... | collective-permute-start | bytes 6291464 | tf_op jit(solution)/shard_map/ppermute | solution.py:722
  427.1 48.7 %collective-permute-start.46 = (bf16[512,2048]{1,0:T(8,128)(2,1)}, bf16[512,2048]{1,0:T(8,128)(2,1)}, u32[]{:S(2)}, u32[]{:S(2)}) collective-permute-start(bf16[512,2048]{1,0:T(8,128)(2,1)} %get-tuple-element.112), channel_id=1, source_target_pairs={{0,4},{4,0},{8,12},{12,8},{16,20},{20,16},{24,28},{28,24},{1,5},{5... | collective-permute-start | bytes 6291464 | tf_op jit(solution)/shard_map/ppermute | solution.py:722
  516.0 47.1 %collective-permute-start.48 = (bf16[512,2048]{1,0:T(8,128)(2,1)}, bf16[512,2048]{1,0:T(8,128)(2,1)}, u32[]{:S(2)}, u32[]{:S(2)}) collective-permute-start(bf16[512,2048]{1,0:T(8,128)(2,1)} %pad_maximum_fusion.1), channel_id=1, source_target_pairs={{0,16},{4,20},{8,0},{12,4},{24,8},{28,12},{16,24},{20,28},{1,17},{... | collective-permute-start | bytes 6291464 | tf_op jit(solution)/shard_map/ppermute | solution.py:718
  603.8 153.1 %all-gather.8.cloned.1.call-start = ((), (), s32[]{:S(2)}) async-start(), calls=%async_computation.9 | async-start | bytes 2621440 | tf_op jit(solution)/shard_map/all_gather | solution.py:382
  603.9 115.4 %collective-permute-start.52 = (bf16[512,2048]{1,0:T(8,128)(2,1)}, bf16[512,2048]{1,0:T(8,128)(2,1)}, u32[]{:S(2)}, u32[]{:S(2)}) collective-permute-start(bf16[512,2048]{1,0:T(8,128)(2,1)} %convolution_convert_fusion.10), channel_id=1, source_target_pairs={{0,4},{4,0},{8,12},{12,8},{16,20},{20,16},{24,28},{28,24},{1,5},{5... | collective-permute-start | bytes 6291464 | tf_op jit(solution)/shard_map/ppermute | solution.py:722
  690.0 219.6 %reduce-scatter.7.cloned.1.call-start = ((), (), s32[]{:S(2)}) async-start(), calls=%async_computation.7 | async-start | bytes 2621440 | tf_op jit(solution)/shard_map/reduce_scatter | solution.py:386
  692.2 59.9 %collective-permute-start.56 = (bf16[512,2048]{1,0:T(8,128)(2,1)}, bf16[512,2048]{1,0:T(8,128)(2,1)S(1)}, u32[]{:S(2)}, u32[]{:S(2)}) collective-permute-start(bf16[512,2048]{1,0:T(8,128)(2,1)} %pad_maximum_fusion.3), channel_id=1, source_target_pairs={{0,16},{4,20},{8,0},{12,4},{24,8},{28,12},{16,24},{20,28},{1,17},{... | collective-permute-start | bytes 6291464 | tf_op jit(solution)/shard_map/ppermute | solution.py:718
  693.1 59.7 %collective-permute-start.59 = (bf16[512,2048]{1,0:T(8,128)(2,1)}, bf16[512,2048]{1,0:T(8,128)(2,1)S(1)}, u32[]{:S(2)}, u32[]{:S(2)}) collective-permute-start(bf16[512,2048]{1,0:T(8,128)(2,1)} %pad_maximum_fusion.4), channel_id=1, source_target_pairs={{0,8},{4,12},{8,24},{12,28},{24,16},{28,20},{16,0},{20,4},{1,9},{5... | collective-permute-start | bytes 6291464 | tf_op jit(solution)/shard_map/ppermute | solution.py:718
  756.6 153.0 %reduce-scatter.11.cloned.1.call-start = ((), (), s32[]{:S(2)}) async-start(), calls=%async_computation.10 | async-start | bytes 2621440 | tf_op jit(solution)/shard_map/reduce_scatter | solution.py:386
  781.1 75.5 %collective-permute-start.93 = (bf16[256,512]{1,0:T(8,128)(2,1)}, bf16[256,512]{1,0:T(8,128)(2,1)}, u32[]{:S(2)}, u32[]{:S(2)}) collective-permute-start(bf16[256,512]{1,0:T(8,128)(2,1)} %get-tuple-element.262), channel_id=1, source_target_pairs={{0,4},{4,0},{8,12},{12,8},{16,20},{20,16},{24,28},{28,24},{1,5},{5... | collective-permute-start | bytes 786440 | tf_op jit(solution)/shard_map/ppermute | solution.py:722
  781.1 76.1 %collective-permute-start.94 = (bf16[256,512]{1,0:T(8,128)(2,1)}, bf16[256,512]{1,0:T(8,128)(2,1)}, u32[]{:S(2)}, u32[]{:S(2)}) collective-permute-start(bf16[256,512]{1,0:T(8,128)(2,1)} %get-tuple-element.261), channel_id=1, source_target_pairs={{0,4},{4,0},{8,12},{12,8},{16,20},{20,16},{24,28},{28,24},{1,5},{5... | collective-permute-start | bytes 786440 | tf_op jit(solution)/shard_map/ppermute | solution.py:722
  (229 other events, 3589.0 us)
Sparse Core Ops, SparseCore 0:
  117.7 41.7 reduce-scatter.4
  161.1 44.8 all-gather.5
  208.1 44.4 all-gather.3
  604.0 41.0 reduce-scatter.8
  690.1 43.2 all-gather.7
  756.7 41.4 reduce-scatter.6
  847.3 42.9 reduce-scatter.10

commit v2 on v1

--- a/solution.py
+++ b/solution.py
@@ -273,7 +273,7 @@
     share = jnp.sum(pick_exp * own_ref[...], axis=0, keepdims=True) / jnp.sum(
         pick_exp, axis=0, keepdims=True
     )
-    step = 32 if hidden % 32 == 0 else 16
+    step = 64 if hidden % 64 == 0 else 16
 
     def body(i, score):
         rows = pl.ds(pl.multiple_of(i * step, step), step)
@@ -765,8 +765,11 @@
 def collect(pairs):
     chips = len(pairs)
     half = pairs[0][0].shape[0] // 2
-    far = add_bf(pairs[chips // 2][0], core_swap(pairs[chips // 2][1]))
-    merged = [add_bf(same, core_swap(other)) for same, other in pairs]
+    others = []
+    for pair in pairs:
+        others.append(core_swap(pair[1]))
+    far = add_bf(pairs[chips // 2][0], others[chips // 2])
+    merged = [add_bf(pair[0], other) for pair, other in zip(pairs, others)]
     carry_back, carry_on = ring_move(far[:half], -1), ring_move(far[half:], 1)
     for step in range(chips // 2 - 1, 0, -1):
         back, on = merged[step], merged[chips - step]
@@ -1024,19 +1027,15 @@
     )[None]
     expert_up_grad = jnp.dot(up_pre_all, rows_all, preferred_element_type=jnp.float32)[None]
     gate_grads, _ = lax.optimization_barrier((gate_grads, routed_back))
-    order = jnp.array(ring_order(dp_count), jnp.int32)
-    dp_place = lax.axis_index("dp")
-    ring_place = jnp.argmax((order == dp_place // 2).astype(jnp.int32)).astype(jnp.int32)
+    _, ring_place, core_here, device_at = ring_neighbours(dp_count)
     gate_grad = jnp.zeros((tokens_here, experts_all), jnp.float32)
     for k, both in enumerate(gate_grads):
-        chip_from = jnp.sum(
-            jnp.where(jnp.arange(chips) == (ring_place + k) % chips, order, 0)
-        )
+        same_from = device_at(ring_place + k)
         for swap in range(2):
             piece = both[0, swap * tokens_here : (swap + 1) * tokens_here]
             if k or swap:
                 piece = direct_move(piece, -k, swap)
-            device_from = 2 * chip_from + (dp_place % 2 if swap == 0 else 1 - dp_place % 2)
+            device_from = same_from + swap * (1 - 2 * core_here)
             expert_from = device_from * experts_group + mp_place // 2
             gate_grad = gate_grad + piece[:, None] * (expert_places == expert_from).astype(
                 jnp.float32
@@ -1062,9 +1061,9 @@
     )
     sdown_grad = weight_grads(grad_late, shared_late[0], places)
     moe_rows_grad = weight_grads(moe_late, jnp.concatenate(shared_late[1:], axis=1), places)
-    shared_back = jnp.dot(
-        shared_gate_pre, sgate_w, preferred_element_type=jnp.float32
-    ) + jnp.dot(shared_up_pre, sup_w, preferred_element_type=jnp.float32)
+    shared_back = jnp.dot(shared_gate_pre, sgate_w, preferred_element_type=jnp.float32)
+    shared_back_up = jnp.dot(shared_up_pre, sup_w, preferred_element_type=jnp.float32)
+    shared_back = shared_back + shared_back_up
     router_mine = lax.dynamic_slice_in_dim(router_back, mp_place * share_width, share_width, axis=1)
     back_share = mp_share(shared_back + routed_back)
     moe_in_grad = back_share + router_mine

time: 930 us -> 925 us (level)
  transfers between devices with their start and end apart: 123 -> 123, of which waited for: 37 -> 36; matrix products, arithmetic and copies ran while one was open for 23% -> 23% of each run, Pallas kernels for 16% -> 16%
where the time goes in v2:
time: 925 us; the launch traced here: 915 us
  waiting for transfers between devices  311 us (34%)
  Pallas kernels  200 us (22%)
  matrix products  145 us (16%)
  starting transfers between devices  101 us (11%)
  other arithmetic  74.1 us (8%)
  local copies, waits for them, and re-layouts  51.8 us (6%)
  between operations  16.7 us (2%)
  blocking collectives  16.4 us (2%)
    ppermute x48, waiting for transfers between devices, ring_move(): return lax.ppermute(values, 'dp', pairs)  246 us
    pallas_call x4, Pallas kernels, expert_rows(): pl.pallas_call(functools.partial(expert_kernel, len(held), k), grid=(2,),...  115 us
    ppermute x48, starting transfers between devices, ring_move(): return lax.ppermute(values, 'dp', pairs)  64.7 us
    pallas_call x1, Pallas kernels, gather_all(): pl.pallas_call(functools.partial(gather_kernel, dp_count, mp_count, tuple...  50.3 us
    all_gather x3, waiting for transfers between devices, full_rows(): return lax.all_gather(piece_rows, 'mp', axis=1, tiled=True)  32.7 us
    dot_general x8, matrix products, out_rows(): jnp.dot(act_late[:, low:low + tokens_here].T, own_down, preferred_element...  30.1 us
    dot_general x1, matrix products, shards(): jnp.dot(gate_pre_all, rows_all, preferred_element_type=jnp.float32)[None]  19.2 us
    dot_general x1, matrix products, shards(): jnp.dot(act_all, grads_all, preferred_element_type=jnp.float32)[None]  19 us
  transfers between devices with their start and end apart: 123, of which 36 were waited for; matrix products, arithmetic and copies ran while one was open for 23% of the time, Pallas kernels for 16%

profile of v2, /device:TPU:0, one launch (start us, length us, event | category | flops | bytes accessed | tf_op | source)
XLA Modules:
  0.0 915.2 jit_solution(5921196729863867996)
XLA Ops:
  10.4 50.3 %gather_all.1 = (bf16[512,2048]{1,0:T(8,128)(2,1)}, bf16[768,2048]{1,0:T(8,128)(2,1)}, bf16[144,2048]{1,0:T(8,128)(2,1)}, bf16[512,1024]{1,0:T(8,128)(2,1)}, bf1...) custom-call(bf16[512,512]{1,0:T(8,128)(2,1)} %refs_0_.1, bf16[768,256]{1,0:T(8,128)(2,1)} %pad_maximum_fusion.12.refs_1_, ...), custom_call_target="tpu_custom_call" | custom-call | bytes 144703488 | tf_op jit(solution)/shard_map/gather_all/pallas_call | solution.py:622
  66.0 16.4 %all_gather.12 = bf16[512,576]{0,1:T(8,128)(2,1)S(1)} all-gather(bf16[512,144]{0,1:T(8,128)(2,1)S(1)} %convolution_convert_fusion.16), channel_id=1, replica_groups=mesh['dp'=8,'mp'=4] {'mp'}, dimensions={1}, use_global_device_ids=true | all-gather | bytes 737280 | tf_op jit(solution)/shard_map/all_gather | solution.py:382
  120.7 20.8 %collective-permute-done.1.refs_2_ = bf16[2112,256]{1,0:T(8,128)(2,1)S(1)} collective-permute-done((bf16[2112,256]{1,0:T(8,128)(2,1)S(1)}, bf16[2112,256]{1,0:T(8,128)(2,1)S(1)}, u32[]{:S(2)}, u32[]{:S(2)}) %collective-permute-start.1) | collective-permute-done | bytes 1081376 | tf_op jit(solution)/shard_map/ppermute | solution.py:718
  143.9 15.4 %reduce-scatter.5.cloned.1.call-done = bf16[512,512]{1,0:T(8,128)(2,1)} async-done(((bf16[512,2048]{1,0:T(8,128)(2,1)}), bf16[512,512]{1,0:T(8,128)(2,1)}) %reduce-scatter.5.cloned.1.call-update) | async-done | bytes 524304 | tf_op jit(solution)/shard_map/reduce_scatter | solution.py:386
  219.8 32.7 %all-gather.4.cloned.1.call-done = bf16[512,2048]{1,0:T(8,128)(2,1)} async-done(((bf16[512,512]{1,0:T(8,128)(2,1)}), bf16[512,2048]{1,0:T(8,128)(2,1)}) %all-gather.4.cloned.1.call-update) | async-done | bytes 2097168 | tf_op jit(solution)/shard_map/all_gather | solution.py:382
  264.1 16.8 %collective-permute-done.12.refs_4_ = bf16[256,2048]{1,0:T(8,128)(2,1)} collective-permute-done((bf16[256,2048]{1,0:T(8,128)(2,1)}, bf16[256,2048]{1,0:T(8,128)(2,1)}, u32[]{:S(2)}, u32[]{:S(2)}) %collective-permute-start.12) | collective-permute-done | bytes 1048608 | tf_op jit(solution)/shard_map/ppermute | solution.py:718
  292.8 14.3 %collective-permute-done.18.refs_0_ = bf16[256,2048]{1,0:T(8,128)(2,1)} collective-permute-done((bf16[256,2048]{1,0:T(8,128)(2,1)S(1)}, bf16[256,2048]{1,0:T(8,128)(2,1)}, u32[]{:S(2)}, u32[]{:S(2)}) %collective-permute-start.18) | collective-permute-done | bytes 1048608 | tf_op jit(solution)/shard_map/ppermute | solution.py:718
  308.6 20.9 %collective-permute-done.32.refs_1_ = bf16[256,2048]{1,0:T(8,128)(2,1)} collective-permute-done((bf16[256,2048]{1,0:T(8,128)(2,1)S(1)}, bf16[256,2048]{1,0:T(8,128)(2,1)}, u32[]{:S(2)}, u32[]{:S(2)}) %collective-permute-start.32) | collective-permute-done | bytes 1048608 | tf_op jit(solution)/shard_map/ppermute | solution.py:718
  331.4 28.5 %expert_rows.4 = (bf16[512,2048]{1,0:T(8,128)(2,1)}, bf16[512,2048]{1,0:T(8,128)(2,1)}, f32[1,1024]{1,0:T(1,128)}, bf16[704,4096]{1,0:T(8,128)(2,1)}, bf16[704,4...) custom-call(bf16[256,2048]{1,0:T(8,128)(2,1)} %copy-done.46, ...), custom_call_target="tpu_custom_call" | custom-call | flops 14763950080 | bytes 29622272 | tf_op jit(solution)/shard_map/expert_rows/pallas_call | solution.py:329
  362.7 28.5 %expert_rows.5 = (bf16[512,2048]{1,0:T(8,128)(2,1)}, bf16[512,2048]{1,0:T(8,128)(2,1)}, f32[1,1024]{1,0:T(1,128)}, bf16[704,4096]{1,0:T(8,128)(2,1)}, bf16[704,4...) custom-call(bf16[256,2048]{1,0:T(8,128)(2,1)} %collective-permute-do, ...), custom_call_target="tpu_custom_call", output_to_operand_aliasing={{3}: (13, {}), {4}: (14, {}), {5}: (15, {}), {6}: (16, {}),... | custom-call | flops 14763950080 | bytes 29622272 | tf_op jit(solution)/shard_map/expert_rows/pallas_call | solution.py:329
  392.5 28.7 %expert_rows.6 = (bf16[512,2048]{1,0:T(8,128)(2,1)}, bf16[512,2048]{1,0:T(8,128)(2,1)}, f32[1,1024]{1,0:T(1,128)}, bf16[704,4096]{1,0:T(8,128)(2,1)}, bf16[704,4...) custom-call(bf16[256,2048]{1,0:T(8,128)(2,1)} %collective-permute-do, ...), custom_call_target="tpu_custom_call", output_to_operand_aliasing={{3}: (13, {}), {4}: (14, {}), {5}: (15, {}), {6}: (16, {}),... | custom-call | flops 14763950080 | bytes 29622272 | tf_op jit(solution)/shard_map/expert_rows/pallas_call | solution.py:329
  422.8 28.9 %expert_rows.7 = (bf16[512,2048]{1,0:T(8,128)(2,1)}, bf16[512,2048]{1,0:T(8,128)(2,1)}, f32[1,1024]{1,0:T(1,128)}, bf16[704,4096]{1,0:T(8,128)(2,1)}, bf16[704,4...) custom-call(bf16[256,2048]{1,0:T(8,128)(2,1)} %collective-permute-do, ...), custom_call_target="tpu_custom_call", output_to_operand_aliasing={{3}: (13, {}), {4}: (14, {}), {5}: (15, {}), {6}: (16, {}),... | custom-call | flops 14763950080 | bytes 29622272 | tf_op jit(solution)/shard_map/expert_rows/pallas_call | solution.py:329
  452.1 19.0 %convolution_bitcast_fusion = f32[1,704,2048]{2,1,0:T(8,128)} fusion(bf16[704,4096]{1,0:T(8,128)(2,1)} %get-tuple-element.114, bf16[4096,2048]{1,0:T(8,128)(2,1)} %get-tuple-element.137), kind=kOutput, calls=%fused_computation.34 | convolution fusion | flops 11811160064 | bytes 28311552 | tf_op jit(solution)/shard_map/dot_general | solution.py:1024
  473.8 11.0 %collective-permute-start.47 = (bf16[256,2048]{1,0:T(8,128)(2,1)S(1)}, bf16[256,2048]{1,0:T(8,128)(2,1)S(1)}, u32[]{:S(2)}, u32[]{:S(2)}) collective-permute-start(bf16[256,2048]{1,0:T(8,128)(2,1)S(1)} %get-tuple-element.262), channel_id=1, source_target_pairs={{0,16},{4,20},{8,0},{12,4},{24,8},{28,12},{16,24},{20,28},{1,17},{... | collective-permute-start | bytes 3145736 | tf_op jit(solution)/shard_map/ppermute | solution.py:718
  488.1 21.2 %collective-permute-done.47 = bf16[256,2048]{1,0:T(8,128)(2,1)S(1)} collective-permute-done((bf16[256,2048]{1,0:T(8,128)(2,1)S(1)}, bf16[256,2048]{1,0:T(8,128)(2,1)S(1)}, u32[]{:S(2)}, u32[]{:S(2)}) %collective-permute-start.47) | collective-permute-done | bytes 1048608 | tf_op jit(solution)/shard_map/ppermute | solution.py:718
  515.3 13.9 %convolution_bitcast_fusion.1 = f32[1,704,2048]{2,1,0:T(8,128)} fusion(bf16[704,4096]{1,0:T(8,128)(2,1)S(1)} %bitcast.130, bf16[4096,2048]{1,0:T(8,128)(2,1)S(1)} %bitcast.128), kind=kOutput, calls=%fused_computation.35 | convolution fusion | flops 11811160064 | bytes 28311552 | tf_op jit(solution)/shard_map/dot_general | solution.py:1028
  529.2 29.2 %collective-permute-done.48 = bf16[512,2048]{1,0:T(8,128)(2,1)} collective-permute-done((bf16[512,2048]{1,0:T(8,128)(2,1)}, bf16[512,2048]{1,0:T(8,128)(2,1)}, u32[]{:S(2)}, u32[]{:S(2)}) %collective-permute-start.48) | collective-permute-done | bytes 2097184 | tf_op jit(solution)/shard_map/ppermute | solution.py:718
  634.3 8.6 collective-permute-done.106
  656.9 17.0 %collective-permute-done.55 = bf16[256,2048]{1,0:T(8,128)(2,1)S(1)} collective-permute-done((bf16[256,2048]{1,0:T(8,128)(2,1)S(1)}, bf16[256,2048]{1,0:T(8,128)(2,1)S(1)}, u32[]{:S(2)}, u32[]{:S(2)}) %collective-permute-start.55) | collective-permute-done | bytes 1048608 | tf_op jit(solution)/shard_map/ppermute | solution.py:718
  688.9 19.2 %convolution_bitcast_fusion.2 = f32[1,704,2048]{2,1,0:T(8,128)} fusion(bf16[704,4096]{1,0:T(8,128)(2,1)} %get-tuple-element.134, bf16[4096,2048]{1,0:T(8,128)(2,1)} %get-tuple-element.135), kind=kOutput, calls=%fused_computation.36 | convolution fusion | flops 11811160064 | bytes 28311552 | tf_op jit(solution)/shard_map/dot_general | solution.py:1025
  717.8 28.9 %collective-permute-done.56 = bf16[512,2048]{1,0:T(8,128)(2,1)S(1)} collective-permute-done((bf16[512,2048]{1,0:T(8,128)(2,1)}, bf16[512,2048]{1,0:T(8,128)(2,1)S(1)}, u32[]{:S(2)}, u32[]{:S(2)}) %collective-permute-start.56) | collective-permute-done | bytes 2097184 | tf_op jit(solution)/shard_map/ppermute | solution.py:718
  761.2 8.7 attend_backward.1
  799.0 10.2 %collective-permute-done.71 = bf16[512,144]{1,0:T(8,128)(2,1)S(1)} collective-permute-done((bf16[512,144]{1,0:T(8,128)(2,1)S(1)}, bf16[512,144]{1,0:T(8,128)(2,1)S(1)}, u32[]{:S(2)}, u32[]{:S(2)}) %collective-permute-start.71) | collective-permute-done | bytes 147488 | tf_op jit(solution)/shard_map/ppermute | solution.py:848
  821.9 11.2 %small_total.1 = f32[36,128]{1,0:T(8,128)} custom-call(f32[36,128]{1,0:T(8,128)} %maximum_bitcast_fusion.4.value_ref), custom_call_target="tpu_custom_call" | custom-call | bytes 4194304 | tf_op jit(solution)/shard_map/small_total/pallas_call | solution.py:690
  (682 shorter events, 398.3 us)
Async XLA Ops:
  7.2 152.1 %reduce-scatter.5.cloned.1.call-start = ((), (), s32[]{:S(2)}) async-start(), calls=%async_computation.4 | async-start | bytes 2621440 | tf_op jit(solution)/shard_map/reduce_scatter | solution.py:386
  117.4 90.7 %all-gather.6.cloned.1.call-start = ((), (), s32[]{:S(2)}) async-start(), calls=%async_computation.6 | async-start | bytes 2621440 | tf_op jit(solution)/shard_map/all_gather | solution.py:382
  118.1 134.3 %all-gather.4.cloned.1.call-start = ((), (), s32[]{:S(2)}) async-start(), calls=%async_computation.5 | async-start | bytes 2621440 | tf_op jit(solution)/shard_map/all_gather | solution.py:382
  161.3 521.0 %reduce-scatter.9.cloned.1.call-start = ((), (), s32[]{:S(2)}) async-start(), calls=%async_computation.8 | async-start | bytes 2621440 | tf_op jit(solution)/shard_map/reduce_scatter | solution.py:386
  211.5 45.8 %collective-permute-start.23 = (bf16[256,2048]{1,0:T(8,128)(2,1)}, bf16[256,2048]{1,0:T(8,128)(2,1)S(1)}, u32[]{:S(2)}, u32[]{:S(2)}) collective-permute-start(bf16[256,2048]{1,0:T(8,128)(2,1)} %get-tuple-element.265.refs_4_), channel_id=1, source_target_pairs={{0,8},{4,12},{8,24},{12,28},{24,16},{28,20},{16,0},{20,4},{1,9},{5... | collective-permute-start | bytes 3145736 | tf_op jit(solution)/shard_map/ppermute | solution.py:718
  213.1 46.6 %collective-permute-start.35 = (bf16[256,2048]{1,0:T(8,128)(2,1)}, bf16[256,2048]{1,0:T(8,128)(2,1)}, u32[]{:S(2)}, u32[]{:S(2)}) collective-permute-start(bf16[256,2048]{1,0:T(8,128)(2,1)} %get-tuple-element.264.refs_5_), channel_id=1, source_target_pairs={{0,8},{4,12},{8,24},{12,28},{24,16},{28,20},{16,0},{20,4},{1,9},{5... | collective-permute-start | bytes 3145736 | tf_op jit(solution)/shard_map/ppermute | solution.py:718
  214.3 49.3 %collective-permute-start.13 = (bf16[256,2048]{1,0:T(8,128)(2,1)}, bf16[256,2048]{1,0:T(8,128)(2,1)S(1)}, u32[]{:S(2)}, u32[]{:S(2)}) collective-permute-start(bf16[256,2048]{1,0:T(8,128)(2,1)} %get-tuple-element.264.refs_5_), channel_id=1, source_target_pairs={{0,16},{4,20},{8,0},{12,4},{24,8},{28,12},{16,24},{20,28},{1,17},{... | collective-permute-start | bytes 3145736 | tf_op jit(solution)/shard_map/ppermute | solution.py:718
  282.4 47.1 %collective-permute-start.32 = (bf16[256,2048]{1,0:T(8,128)(2,1)S(1)}, bf16[256,2048]{1,0:T(8,128)(2,1)}, u32[]{:S(2)}, u32[]{:S(2)}) collective-permute-start(bf16[256,2048]{1,0:T(8,128)(2,1)S(1)} %get-tuple-element.266.refs_1_), channel_id=1, source_target_pairs={{0,8},{4,12},{8,24},{12,28},{24,16},{28,20},{16,0},{20,4},{1,9},{5... | collective-permute-start | bytes 3145736 | tf_op jit(solution)/shard_map/ppermute | solution.py:718
  292.3 67.7 %collective-permute-start.25 = (bf16[256,2048]{1,0:T(8,128)(2,1)S(1)}, bf16[256,2048]{1,0:T(8,128)(2,1)S(1)}, u32[]{:S(2)}, u32[]{:S(2)}) collective-permute-start(bf16[256,2048]{1,0:T(8,128)(2,1)S(1)} %collective-permute-done.13.refs_5_), channel_id=1, source_target_pairs={{0,16},{4,20},{8,0},{12,4},{24,8},{28,12},{16,24},{20,28},{1,17},{... | collective-permute-start | bytes 3145736 | tf_op jit(solution)/shard_map/ppermute | solution.py:718
  307.0 53.2 %collective-permute-start.33 = (bf16[256,2048]{1,0:T(8,128)(2,1)}, bf16[256,2048]{1,0:T(8,128)(2,1)}, u32[]{:S(2)}, u32[]{:S(2)}) collective-permute-start(bf16[256,2048]{1,0:T(8,128)(2,1)} %collective-permute-done.18.refs_0_), channel_id=1, source_target_pairs={{0,4},{4,0},{8,12},{12,8},{16,20},{20,16},{24,28},{28,24},{1,5},{5... | collective-permute-start | bytes 3145736 | tf_op jit(solution)/shard_map/ppermute | solution.py:722
  307.0 55.2 %collective-permute-start.19 = (bf16[256,2048]{1,0:T(8,128)(2,1)}, bf16[256,2048]{1,0:T(8,128)(2,1)}, u32[]{:S(2)}, u32[]{:S(2)}) collective-permute-start(bf16[256,2048]{1,0:T(8,128)(2,1)} %collective-permute-done.18.refs_0_), channel_id=1, source_target_pairs={{0,8},{4,12},{8,24},{12,28},{24,16},{28,20},{16,0},{20,4},{1,9},{5... | collective-permute-start | bytes 3145736 | tf_op jit(solution)/shard_map/ppermute | solution.py:718
  391.9 137.3 %collective-permute-start.44 = (bf16[512,2048]{1,0:T(8,128)(2,1)}, bf16[512,2048]{1,0:T(8,128)(2,1)}, u32[]{:S(2)}, u32[]{:S(2)}) collective-permute-start(bf16[512,2048]{1,0:T(8,128)(2,1)} %get-tuple-element.107), channel_id=1, source_target_pairs={{0,4},{4,0},{8,12},{12,8},{16,20},{20,16},{24,28},{28,24},{1,5},{5... | collective-permute-start | bytes 6291464 | tf_op jit(solution)/shard_map/ppermute | solution.py:722
  422.3 62.5 %collective-permute-start.45 = (bf16[512,2048]{1,0:T(8,128)(2,1)}, bf16[512,2048]{1,0:T(8,128)(2,1)S(1)}, u32[]{:S(2)}, u32[]{:S(2)}) collective-permute-start(bf16[512,2048]{1,0:T(8,128)(2,1)} %get-tuple-element.109), channel_id=1, source_target_pairs={{0,4},{4,0},{8,12},{12,8},{16,20},{20,16},{24,28},{28,24},{1,5},{5... | collective-permute-start | bytes 6291464 | tf_op jit(solution)/shard_map/ppermute | solution.py:722
  422.7 48.4 %collective-permute-start.46 = (bf16[512,2048]{1,0:T(8,128)(2,1)}, bf16[512,2048]{1,0:T(8,128)(2,1)}, u32[]{:S(2)}, u32[]{:S(2)}) collective-permute-start(bf16[512,2048]{1,0:T(8,128)(2,1)} %get-tuple-element.111), channel_id=1, source_target_pairs={{0,4},{4,0},{8,12},{12,8},{16,20},{20,16},{24,28},{28,24},{1,5},{5... | collective-permute-start | bytes 6291464 | tf_op jit(solution)/shard_map/ppermute | solution.py:722
  511.3 47.1 %collective-permute-start.48 = (bf16[512,2048]{1,0:T(8,128)(2,1)}, bf16[512,2048]{1,0:T(8,128)(2,1)}, u32[]{:S(2)}, u32[]{:S(2)}) collective-permute-start(bf16[512,2048]{1,0:T(8,128)(2,1)} %pad_maximum_fusion.1), channel_id=1, source_target_pairs={{0,16},{4,20},{8,0},{12,4},{24,8},{28,12},{16,24},{20,28},{1,17},{... | collective-permute-start | bytes 6291464 | tf_op jit(solution)/shard_map/ppermute | solution.py:718
  513.8 46.8 %collective-permute-start.51 = (bf16[512,2048]{1,0:T(8,128)(2,1)}, bf16[512,2048]{1,0:T(8,128)(2,1)}, u32[]{:S(2)}, u32[]{:S(2)}) collective-permute-start(bf16[512,2048]{1,0:T(8,128)(2,1)} %pad_maximum_fusion.2), channel_id=1, source_target_pairs={{0,8},{4,12},{8,24},{12,28},{24,16},{28,20},{16,0},{20,4},{1,9},{5... | collective-permute-start | bytes 6291464 | tf_op jit(solution)/shard_map/ppermute | solution.py:718
  598.2 153.1 %all-gather.8.cloned.1.call-start = ((), (), s32[]{:S(2)}) async-start(), calls=%async_computation.9 | async-start | bytes 2621440 | tf_op jit(solution)/shard_map/all_gather | solution.py:382
  598.2 115.8 %collective-permute-start.52 = (bf16[512,2048]{1,0:T(8,128)(2,1)}, bf16[512,2048]{1,0:T(8,128)(2,1)}, u32[]{:S(2)}, u32[]{:S(2)}) collective-permute-start(bf16[512,2048]{1,0:T(8,128)(2,1)} %convolution_convert_fusion.10), channel_id=1, source_target_pairs={{0,4},{4,0},{8,12},{12,8},{16,20},{20,16},{24,28},{28,24},{1,5},{5... | collective-permute-start | bytes 6291464 | tf_op jit(solution)/shard_map/ppermute | solution.py:722
  684.6 220.2 %reduce-scatter.7.cloned.1.call-start = ((), (), s32[]{:S(2)}) async-start(), calls=%async_computation.7 | async-start | bytes 2621440 | tf_op jit(solution)/shard_map/reduce_scatter | solution.py:386
  686.8 59.9 %collective-permute-start.56 = (bf16[512,2048]{1,0:T(8,128)(2,1)}, bf16[512,2048]{1,0:T(8,128)(2,1)S(1)}, u32[]{:S(2)}, u32[]{:S(2)}) collective-permute-start(bf16[512,2048]{1,0:T(8,128)(2,1)} %pad_maximum_fusion.3), channel_id=1, source_target_pairs={{0,16},{4,20},{8,0},{12,4},{24,8},{28,12},{16,24},{20,28},{1,17},{... | collective-permute-start | bytes 6291464 | tf_op jit(solution)/shard_map/ppermute | solution.py:718
  687.4 59.8 %collective-permute-start.59 = (bf16[512,2048]{1,0:T(8,128)(2,1)}, bf16[512,2048]{1,0:T(8,128)(2,1)S(1)}, u32[]{:S(2)}, u32[]{:S(2)}) collective-permute-start(bf16[512,2048]{1,0:T(8,128)(2,1)} %pad_maximum_fusion.4), channel_id=1, source_target_pairs={{0,8},{4,12},{8,24},{12,28},{24,16},{28,20},{16,0},{20,4},{1,9},{5... | collective-permute-start | bytes 6291464 | tf_op jit(solution)/shard_map/ppermute | solution.py:718
  751.0 153.8 %reduce-scatter.11.cloned.1.call-start = ((), (), s32[]{:S(2)}) async-start(), calls=%async_computation.10 | async-start | bytes 2621440 | tf_op jit(solution)/shard_map/reduce_scatter | solution.py:386
  775.5 76.3 %collective-permute-start.93 = (bf16[256,512]{1,0:T(8,128)(2,1)}, bf16[256,512]{1,0:T(8,128)(2,1)}, u32[]{:S(2)}, u32[]{:S(2)}) collective-permute-start(bf16[256,512]{1,0:T(8,128)(2,1)} %get-tuple-element.256), channel_id=1, source_target_pairs={{0,4},{4,0},{8,12},{12,8},{16,20},{20,16},{24,28},{28,24},{1,5},{5... | collective-permute-start | bytes 786440 | tf_op jit(solution)/shard_map/ppermute | solution.py:722
  775.5 76.8 %collective-permute-start.94 = (bf16[256,512]{1,0:T(8,128)(2,1)}, bf16[256,512]{1,0:T(8,128)(2,1)}, u32[]{:S(2)}, u32[]{:S(2)}) collective-permute-start(bf16[256,512]{1,0:T(8,128)(2,1)} %get-tuple-element.255), channel_id=1, source_target_pairs={{0,4},{4,0},{8,12},{12,8},{16,20},{20,16},{24,28},{28,24},{1,5},{5... | collective-permute-start | bytes 786440 | tf_op jit(solution)/shard_map/ppermute | solution.py:722
  (228 other events, 3524.6 us)
Sparse Core Ops, SparseCore 0:
  117.5 41.7 reduce-scatter.4
  160.9 44.8 all-gather.5
  207.9 44.4 all-gather.3
  598.3 41.9 reduce-scatter.8
  684.7 43.4 all-gather.7
  751.1 42.3 reduce-scatter.6
  842.5 42.9 reduce-scatter.10
